TPU v7x, 32 devices: a whole 2x2x4 slice. The times are simulated.
32 devices in a mesh: gx: 4 (over y, x), gy: 4 (over z), gz: 2 (over core).
Axes of the slice: x: 2, y: 2, z: 4, core: 2. Of those that a mesh axis runs over, the one named last changes fastest.
Arguments:
- right_side: float32 [5, 512, 8, 128], P(None, ('gx', 'gy', 'gz')), may hold values from -6 to 6
- diag_inverse: bfloat16 [5, 512, 128, 128], P(None, ('gx', 'gy', 'gz')), may hold values from -0.5 to 0.5
- off_blocks: bfloat16 [4, 1024, 128, 128], P(None, ('gx', 'gy', 'gz')), may hold values from -0.375 to 0.375
- live_counts: int32 [5, 32], P(None, ('gx', 'gy', 'gz')), may hold values from 1 to 16, as said below
- source_slot: int32 [4, 1024], P(None, ('gx', 'gy', 'gz')), may hold values from 0 to 15, as said below
- target_owner: int32 [4, 1024], P(None, ('gx', 'gy', 'gz')), may hold values from 0 to 31, as said below
- target_block: int32 [4, 1024], P(None, ('gx', 'gy', 'gz')), may hold values from 16 to 79, as said below
Outputs:
- solution: float32 [5, 512, 8, 128], P(None, ('gx', 'gy', 'gz'))
Inputs may be any that keep to these rules, and one draw needn't show every extreme that they name: `live_counts`: slots at or past a device's count in a level are empty; in every level some device has all 16 slots live. `source_slot`: names a live slot of the issuing device in the same level. `target_owner`: in every level, each device's records go exactly 2 each to 16 distinct owners and none to the others. `target_block`: the level part is later than the record's own level, and the slot is live at the owner in that level.
All inputs are finite; a program needn't handle non-finite values.
Results may differ from a plain program's by a relative error of at most 0.013.
Values sent between devices are 32-bit elements; how exact they have to be, the bound alone decides.
No kernel may reach another device: no remote copies, remote signals or barrier semaphores. Data moves between devices by JAX's collectives and lax.ppermute only.
A program may use at most 64 MiB of HBM per device.

v0:
```python
import jax
import jax.numpy as jnp
from jax import lax
from jax.sharding import PartitionSpec as P

CAP = 2


def shards(
    right_side, diag_inverse, off_blocks, live_counts, source_slot, target_owner, target_block
):
    levels_total = right_side.shape[0]
    slots = right_side.shape[1]
    rhs_count = right_side.shape[2]
    width = right_side.shape[3]
    flat_width = rhs_count * width
    records = off_blocks.shape[1]
    owners = lax.axis_size(("gx", "gy", "gz"))
    slot_ids = jnp.arange(slots, dtype=jnp.int32)
    owner_ids = jnp.arange(owners, dtype=jnp.int32)
    buffer_ids = jnp.arange(owners * CAP, dtype=jnp.int32)
    block_ids = jnp.arange(levels_total * slots, dtype=jnp.int32)
    accumulated = jnp.zeros((levels_total * slots, flat_width), jnp.float32)
    results = []
    for level_at in range(levels_total):
        pending = accumulated[level_at * slots : (level_at + 1) * slots].reshape(
            slots, rhs_count, width
        )
        work_rows = (right_side[level_at] - pending).astype(jnp.bfloat16)
        solved = jnp.einsum(
            "srb,sbc->src", work_rows, diag_inverse[level_at], preferred_element_type=jnp.float32
        )
        solved = jnp.where(
            (slot_ids < live_counts[level_at, 0])[:, None, None], solved, jnp.float32(0.0)
        )
        results.append(solved)
        if level_at + 1 < levels_total:
            rounded = solved.astype(jnp.bfloat16)
            picker = (source_slot[level_at][:, None] == slot_ids[None, :]).astype(jnp.bfloat16)
            picked = jnp.einsum(
                "ks,srb->krb", picker, rounded, preferred_element_type=jnp.float32
            ).astype(jnp.bfloat16)
            contribution = jnp.einsum(
                "krb,kbc->krc", picked, off_blocks[level_at], preferred_element_type=jnp.float32
            )
            contribution = contribution.reshape(records, flat_width)
            owners_now = target_owner[level_at]
            blocks_now = target_block[level_at]
            owner_hits = (owners_now[:, None] == owner_ids[None, :]).astype(jnp.int32)
            position = jnp.sum(jnp.cumsum(owner_hits, axis=0) * owner_hits, axis=1) - 1
            slot_of = owners_now * CAP + position
            packer = buffer_ids[:, None] == slot_of[None, :]
            outgoing = jnp.dot(
                packer.astype(jnp.float32), contribution, precision=lax.Precision.HIGHEST
            )
            labels = jnp.sum(packer.astype(jnp.int32) * (blocks_now + 1)[None, :], axis=1) - 1
            arrived, received_labels = (
                lax.all_to_all(
                    outgoing.reshape(owners, CAP, flat_width),
                    ("gx", "gy", "gz"),
                    split_axis=0,
                    concat_axis=0,
                    tiled=True,
                ),
                lax.all_to_all(
                    labels.reshape(owners, CAP),
                    ("gx", "gy", "gz"),
                    split_axis=0,
                    concat_axis=0,
                    tiled=True,
                ),
            )
            arrived = arrived.reshape(owners * CAP, flat_width)
            received_labels = received_labels.reshape(owners * CAP)
            placer = (block_ids[:, None] == received_labels[None, :]).astype(jnp.float32)
            accumulated = accumulated + jnp.dot(placer, arrived, precision=lax.Precision.HIGHEST)
    return jnp.stack(results)


def solution(mesh):
    in_specs = (
        P(None, ("gx", "gy", "gz"), None, None),
        P(None, ("gx", "gy", "gz"), None, None),
        P(None, ("gx", "gy", "gz"), None, None),
        P(None, ("gx", "gy", "gz")),
        P(None, ("gx", "gy", "gz")),
        P(None, ("gx", "gy", "gz")),
        P(None, ("gx", "gy", "gz")),
    )
    out_specs = P(None, ("gx", "gy", "gz"), None, None)
    return jax.shard_map(shards, mesh=mesh, in_specs=in_specs, out_specs=out_specs, check_vma=False)
```

profile of v0, /device:TPU:1, one launch (start us, length us, event | category | flops | bytes accessed | tf_op | source)
XLA Modules:
  0.0 117.2 jit_solution(17567609547212547136)
XLA Ops:
  0.0 0.7 slice_bitcast_fusion.7
  0.7 1.3 %add_bitcast_fusion = (s32[32]{0:T(128)}, s32[32]{0:T(128)S(1)}, s32[32]{0:T(128)S(1)}, s32[32]{0:T(128)S(1)}) fusion(s32[4,32]{1,0:T(4,128)} %param.13), kind=kLoop, calls=%fused_computation.130 | loop fusion | flops 128 | bytes 1024 | tf_op jit(solution)/shard_map/mul | solution.py:56
  2.3 1.3 %fusion.77 = (s32[32]{0:T(128)}, s32[32]{0:T(128)S(1)}, s32[32]{0:T(128)S(1)}, s32[32]{0:T(128)S(1)}) fusion(s32[32]{0:T(128)S(1)} %select_reduce_fusion.1, s32[4,32]{1,0:T(4,128)} %param.12), kind=kLoop, calls=%fused_computation.122 | loop fusion | flops 96 | bytes 1152 | tf_op jit(solution)/shard_map/eq | solution.py:52
  4.4 0.8 fusion.78
  5.3 0.7 sub.55
  6.0 7.1 %all-to-all-start = ((s32[32,1,2]{2,1,0:T(1,128)}), s32[32,1,2]{2,1,0:T(1,128)S(1)}, u32[]{:S(2)}, u32[]{:S(2)}) async-start(s32[32,1,2]{2,1,0:T(1,128)} %bitcast.10), calls=%async_computation | async-start | bytes 32768 | tf_op jit(solution)/shard_map/all_to_all | solution.py:65
  13.1 1.4 %slice_bitcast_fusion.3 = (s32[32]{0:T(128)}, s32[32]{0:T(128)S(1)}, s32[32]{0:T(128)S(1)}, s32[32]{0:T(128)}) fusion(s32[4,32]{1,0:T(4,128)} %param.11), kind=kLoop, calls=%fused_computation.129 | loop fusion | bytes 1024 | tf_op jit(solution)/shard_map/eq | solution.py:39
  14.6 1.5 %fusion.81 = (s32[1,1]{0,1:T(1,128)}, s32[1,1]{0,1:T(1,128)}, s32[1,1]{0,1:T(1,128)}, s32[1,1]{0,1:T(1,128)}, s32[1,1]{0,1:T(1,128)}) fusion(s32[5,1]{0,1:T(1,128)} %param.10), kind=kLoop, calls=%fused_computation.150 | loop fusion | bytes 40 | tf_op jit(solution)/shard_map/slice | solution.py:34
  16.1 0.7 iota_compare_fusion.24
  16.7 2.1 %bitcast_dynamic-update-slice_fusion.3 = (f32[5,16,8,128]{3,2,1,0:T(8,128)}, bf16[16,8,128]{2,1,0:T(8,128)(2,1)S(1)}) fusion(bf16[5,16,128,128]{3,2,1,0:T(8,128)(2,1)} %param.8, f32[5,16,8,128]{3,2,1,0:T(8,128)} %param.7, pred[16]{0:T(512)(128)(4,1)S(1)} %iota_compare_fusion.24), kind=kOutput, calls=%fused_computation.52 | convolution fusion | flops 4227071 | bytes 655376 | tf_op jit(solution)/shard_map/srb,sbc->src/dot_general | solution.py:30
  18.8 0.2 convolution_convert_fusion.3
  19.1 1.6 %fusion.8 = f32[32,8,128]{2,1,0:T(8,128)S(1)} fusion(bf16[4,32,128,128]{3,2,1,0:T(8,128)(2,1)} %param.9, bf16[32,8,128]{2,0,1:T(8,128)(2,1)S(1)} %convolution_convert_fusion.3), kind=kOutput, calls=%fused_computation.19 | convolution fusion | flops 8388608 | bytes 1245184 | tf_op jit(solution)/shard_map/krb,kbc->krc/dot_general | solution.py:43
  20.7 0.3 fusion.47
  21.0 0.9 copy.31
  21.9 5.8 %all-to-all-start.1 = ((f32[32,2,1024]{2,1,0:T(2,128)}), f32[32,2,1024]{2,1,0:T(2,128)S(1)}, u32[]{:S(2)}, u32[]{:S(2)}) async-start(f32[32,2,1024]{2,1,0:T(2,128)} %copy.31), calls=%async_computation.1 | async-start | bytes 524288 | tf_op jit(solution)/shard_map/all_to_all | solution.py:58
  27.9 0.7 sub.60
  28.6 0.6 iota_compare_fusion.23
  29.2 0.5 broadcast.234
  29.7 0.7 reduce.12
  30.5 7.7 %all-to-all-done.1 = f32[32,2,1024]{2,1,0:T(2,128)S(1)} async-done(((f32[32,2,1024]{2,1,0:T(2,128)}), f32[32,2,1024]{2,1,0:T(2,128)S(1)}, u32[]{:S(2)}, u32[]{:S(2)}) %all-to-all-start.1) | async-done | bytes 262176 | tf_op jit(solution)/shard_map/all_to_all | solution.py:58
  38.3 2.4 %all-to-all-start.2 = ((s32[32,1,2]{2,1,0:T(1,128)}), s32[32,1,2]{2,1,0:T(1,128)S(1)}, u32[]{:S(2)}, u32[]{:S(2)}) async-start(s32[32,1,2]{2,1,0:T(1,128)} %bitcast.22), calls=%async_computation.2 | async-start | bytes 32768 | tf_op jit(solution)/shard_map/all_to_all | solution.py:65
  40.8 0.3 fusion.33
  41.2 0.9 fusion.27
  42.0 0.9 bitcast_dynamic-update-slice_fusion.2
  42.9 0.2 convolution_convert_fusion.2
  43.1 1.6 %fusion.6 = f32[32,8,128]{2,1,0:T(8,128)S(1)} fusion(bf16[4,32,128,128]{3,2,1,0:T(8,128)(2,1)} %param.9, bf16[32,8,128]{2,0,1:T(8,128)(2,1)S(1)} %convolution_convert_fusion.2), kind=kOutput, calls=%fused_computation.17 | convolution fusion | flops 8388608 | bytes 1245184 | tf_op jit(solution)/shard_map/krb,kbc->krc/dot_general | solution.py:43
  44.8 0.3 fusion.45
  45.1 0.9 copy.35
  46.0 1.4 %all-to-all-done.2 = s32[32,1,2]{2,1,0:T(1,128)S(1)} async-done(((s32[32,1,2]{2,1,0:T(1,128)}), s32[32,1,2]{2,1,0:T(1,128)S(1)}, u32[]{:S(2)}, u32[]{:S(2)}) %all-to-all-start.2) | async-done | bytes 288 | tf_op jit(solution)/shard_map/all_to_all | solution.py:65
  47.4 4.4 %all-to-all-start.3 = ((f32[32,2,1024]{2,1,0:T(2,128)}), f32[32,2,1024]{2,1,0:T(2,128)S(1)}, u32[]{:S(2)}, u32[]{:S(2)}) async-start(f32[32,2,1024]{2,1,0:T(2,128)} %copy.35), calls=%async_computation.3 | async-start | bytes 524288 | tf_op jit(solution)/shard_map/all_to_all | solution.py:58
  52.0 0.7 sub.65
  52.7 1.2 %iota_compare_fusion.22 = pred[16]{0:T(512)(128)(4,1)} fusion(s32[]{:T(128)} %bitcast.16), kind=kLoop, calls=%fused_computation.137 | loop fusion | flops 16 | bytes 20 | tf_op jit(solution)/shard_map/lt | solution.py:34
  53.9 0.7 reduce.13
  54.5 0.7 eq.333
  55.2 7.1 %all-to-all-done.3 = f32[32,2,1024]{2,1,0:T(2,128)S(1)} async-done(((f32[32,2,1024]{2,1,0:T(2,128)}), f32[32,2,1024]{2,1,0:T(2,128)S(1)}, u32[]{:S(2)}, u32[]{:S(2)}) %all-to-all-start.3) | async-done | bytes 262176 | tf_op jit(solution)/shard_map/all_to_all | solution.py:58
  62.3 2.4 %all-to-all-start.4 = ((s32[32,1,2]{2,1,0:T(1,128)}), s32[32,1,2]{2,1,0:T(1,128)S(1)}, u32[]{:S(2)}, u32[]{:S(2)}) async-start(s32[32,1,2]{2,1,0:T(1,128)} %bitcast.34), calls=%async_computation.4 | async-start | bytes 32768 | tf_op jit(solution)/shard_map/all_to_all | solution.py:65
  64.9 1.0 convolution_add_fusion.1
  66.0 0.9 fusion.26
  66.8 1.5 %bitcast_dynamic-update-slice_fusion.1 = (f32[5,16,8,128]{3,2,1,0:T(8,128)}, bf16[16,8,128]{2,1,0:T(8,128)(2,1)S(1)}) fusion(f32[5,16,8,128]{3,2,1,0:T(8,128)} %get-tuple-element.27, bf16[16,8,128]{2,1,0:T(8,128)(2,1)S(1)} %fusion.26, bf16[5,16,128,128]{3,2,1,0:T(8,128)(2,1)S(1)} %copy-done, pred[16]{0:T(512)(128)(4,1)} %iota_compare_fusion.22), kind=kOutput, calls=%fused_computation.50 | convolution fusion | flops 4227072 | bytes 655872 | tf_op jit(solution)/shard_map/srb,sbc->src/dot_general | solution.py:30
  68.3 0.8 convolution_convert_fusion.1
  69.1 1.6 %fusion.4 = f32[32,8,128]{2,1,0:T(8,128)S(1)} fusion(bf16[4,32,128,128]{3,2,1,0:T(8,128)(2,1)} %param.9, bf16[32,8,128]{2,0,1:T(8,128)(2,1)S(1)} %convolution_convert_fusion.1), kind=kOutput, calls=%fused_computation.15 | convolution fusion | flops 8388608 | bytes 1245184 | tf_op jit(solution)/shard_map/krb,kbc->krc/dot_general | solution.py:43
  70.8 0.3 fusion.43
  71.1 0.9 copy.39
  72.0 5.8 %all-to-all-start.5 = ((f32[32,2,1024]{2,1,0:T(2,128)}), f32[32,2,1024]{2,1,0:T(2,128)S(1)}, u32[]{:S(2)}, u32[]{:S(2)}) async-start(f32[32,2,1024]{2,1,0:T(2,128)} %copy.39), calls=%async_computation.5 | async-start | bytes 524288 | tf_op jit(solution)/shard_map/all_to_all | solution.py:58
  78.0 0.7 sub.70
  78.7 1.1 iota_compare_fusion.21
  79.8 0.7 reduce.14
  80.5 0.7 eq.351
  81.1 7.2 %all-to-all-done.5 = f32[32,2,1024]{2,1,0:T(2,128)S(1)} async-done(((f32[32,2,1024]{2,1,0:T(2,128)}), f32[32,2,1024]{2,1,0:T(2,128)S(1)}, u32[]{:S(2)}, u32[]{:S(2)}) %all-to-all-start.5) | async-done | bytes 262176 | tf_op jit(solution)/shard_map/all_to_all | solution.py:58
  88.3 2.4 %all-to-all-start.6 = ((s32[32,1,2]{2,1,0:T(1,128)}), s32[32,1,2]{2,1,0:T(1,128)S(1)}, u32[]{:S(2)}, u32[]{:S(2)}) async-start(s32[32,1,2]{2,1,0:T(1,128)} %bitcast.46), calls=%async_computation.6 | async-start | bytes 32768 | tf_op jit(solution)/shard_map/all_to_all | solution.py:65
  90.9 0.9 convolution_add_fusion
  91.9 0.9 fusion.25
  92.7 1.5 %bitcast_dynamic-update-slice_fusion = (f32[5,16,8,128]{3,2,1,0:T(8,128)}, bf16[16,8,128]{2,1,0:T(8,128)(2,1)S(1)}) fusion(f32[5,16,8,128]{3,2,1,0:T(8,128)} %get-tuple-element.29, bf16[16,8,128]{2,1,0:T(8,128)(2,1)S(1)} %fusion.25, bf16[5,16,128,128]{3,2,1,0:T(8,128)(2,1)S(1)} %copy-done, pred[16]{0:T(512)(128)(4,1)} %iota_compare_fusion.21), kind=kOutput, calls=%fused_computation.49 | convolution fusion | flops 4227072 | bytes 655872 | tf_op jit(solution)/shard_map/srb,sbc->src/dot_general | solution.py:30
  94.2 0.9 convolution_convert_fusion
  95.1 1.6 %fusion.2 = f32[32,8,128]{2,1,0:T(8,128)S(1)} fusion(bf16[4,32,128,128]{3,2,1,0:T(8,128)(2,1)} %param.9, bf16[32,8,128]{2,0,1:T(8,128)(2,1)S(1)} %convolution_convert_fusion), kind=kOutput, calls=%fused_computation.13 | convolution fusion | flops 8388608 | bytes 1245184 | tf_op jit(solution)/shard_map/krb,kbc->krc/dot_general | solution.py:43
  96.7 1.0 fusion.41
  97.7 0.9 copy.43
  98.6 5.8 %all-to-all-start.7 = ((f32[32,2,1024]{2,1,0:T(2,128)}), f32[32,2,1024]{2,1,0:T(2,128)S(1)}, u32[]{:S(2)}, u32[]{:S(2)}) async-start(f32[32,2,1024]{2,1,0:T(2,128)} %copy.43), calls=%async_computation.7 | async-start | bytes 524288 | tf_op jit(solution)/shard_map/all_to_all | solution.py:58
  104.5 0.7 iota_compare_fusion.20
  105.2 0.7 reduce.15
  106.0 9.0 %all-to-all-done.7 = f32[32,2,1024]{2,1,0:T(2,128)S(1)} async-done(((f32[32,2,1024]{2,1,0:T(2,128)}), f32[32,2,1024]{2,1,0:T(2,128)S(1)}, u32[]{:S(2)}, u32[]{:S(2)}) %all-to-all-start.7) | async-done | bytes 262176 | tf_op jit(solution)/shard_map/all_to_all | solution.py:58
  115.2 0.3 fusion.34
  115.5 0.9 fusion.24
  116.3 0.9 fusion.1
  (55 shorter events, 2.7 us)
Async XLA Ops:
  5.2 46.6 %copy-start.4 = (s32[32]{0:T(128)}, s32[32]{0:T(128)S(1)}, u32[]{:S(2)}) copy-start(s32[32]{0:T(128)S(1)} %get-tuple-element.17) | copy-start | bytes 388
  6.0 15.9 %all-to-all-start = ((s32[32,1,2]{2,1,0:T(1,128)}), s32[32,1,2]{2,1,0:T(1,128)S(1)}, u32[]{:S(2)}, u32[]{:S(2)}) async-start(s32[32,1,2]{2,1,0:T(1,128)} %bitcast.10), calls=%async_computation | async-start | bytes 32768 | tf_op jit(solution)/shard_map/all_to_all | solution.py:65
  13.1 31.6 %copy-start.1 = (s32[32,2]{0,1:T(2,128)}, s32[32,2]{0,1:T(2,128)S(1)}, u32[]{:S(2)}) copy-start(s32[32,2]{0,1:T(2,128)S(1)} %multiply_add_fusion) | copy-start | bytes 772
  16.7 25.3 %copy-start = (bf16[5,16,128,128]{3,2,1,0:T(8,128)(2,1)S(1)}, bf16[5,16,128,128]{3,2,1,0:T(8,128)(2,1)}, u32[]{:S(2)}) copy-start(bf16[5,16,128,128]{3,2,1,0:T(8,128)(2,1)} %param.8) | copy-start | bytes 7864324
  21.9 16.3 %all-to-all-start.1 = ((f32[32,2,1024]{2,1,0:T(2,128)}), f32[32,2,1024]{2,1,0:T(2,128)S(1)}, u32[]{:S(2)}, u32[]{:S(2)}) async-start(f32[32,2,1024]{2,1,0:T(2,128)} %copy.31), calls=%async_computation.1 | async-start | bytes 524288 | tf_op jit(solution)/shard_map/all_to_all | solution.py:58
  38.3 9.2 %all-to-all-start.2 = ((s32[32,1,2]{2,1,0:T(1,128)}), s32[32,1,2]{2,1,0:T(1,128)S(1)}, u32[]{:S(2)}, u32[]{:S(2)}) async-start(s32[32,1,2]{2,1,0:T(1,128)} %bitcast.22), calls=%async_computation.2 | async-start | bytes 32768 | tf_op jit(solution)/shard_map/all_to_all | solution.py:65
  47.4 14.9 %all-to-all-start.3 = ((f32[32,2,1024]{2,1,0:T(2,128)}), f32[32,2,1024]{2,1,0:T(2,128)S(1)}, u32[]{:S(2)}, u32[]{:S(2)}) async-start(f32[32,2,1024]{2,1,0:T(2,128)} %copy.35), calls=%async_computation.3 | async-start | bytes 524288 | tf_op jit(solution)/shard_map/all_to_all | solution.py:58
  62.3 9.7 %all-to-all-start.4 = ((s32[32,1,2]{2,1,0:T(1,128)}), s32[32,1,2]{2,1,0:T(1,128)S(1)}, u32[]{:S(2)}, u32[]{:S(2)}) async-start(s32[32,1,2]{2,1,0:T(1,128)} %bitcast.34), calls=%async_computation.4 | async-start | bytes 32768 | tf_op jit(solution)/shard_map/all_to_all | solution.py:65
  65.9 4.9 %copy-start.2 = (s32[32,2]{0,1:T(2,128)S(1)}, s32[32,2]{0,1:T(2,128)}, u32[]{:S(2)}) copy-start(s32[32,2]{0,1:T(2,128)} %copy-done.1) | copy-start | bytes 772
  65.9 4.9 %copy-start.5 = (s32[32]{0:T(128)S(1)}, s32[32]{0:T(128)}, u32[]{:S(2)}) copy-start(s32[32]{0:T(128)} %copy-done.4) | copy-start | bytes 388
  65.9 11.9 %copy-start.3 = (s32[32]{0:T(128)S(1)}, s32[32]{0:T(128)}, u32[]{:S(2)}) copy-start(s32[32]{0:T(128)} %get-tuple-element.9) | copy-start | bytes 388
  65.9 11.9 %copy-start.6 = (s32[32]{0:T(128)S(1)}, s32[32]{0:T(128)}, u32[]{:S(2)}) copy-start(s32[32]{0:T(128)} %get-tuple-element.5) | copy-start | bytes 388
  72.0 16.3 %all-to-all-start.5 = ((f32[32,2,1024]{2,1,0:T(2,128)}), f32[32,2,1024]{2,1,0:T(2,128)S(1)}, u32[]{:S(2)}, u32[]{:S(2)}) async-start(f32[32,2,1024]{2,1,0:T(2,128)} %copy.39), calls=%async_computation.5 | async-start | bytes 524288 | tf_op jit(solution)/shard_map/all_to_all | solution.py:58
  88.3 10.3 %all-to-all-start.6 = ((s32[32,1,2]{2,1,0:T(1,128)}), s32[32,1,2]{2,1,0:T(1,128)S(1)}, u32[]{:S(2)}, u32[]{:S(2)}) async-start(s32[32,1,2]{2,1,0:T(1,128)} %bitcast.46), calls=%async_computation.6 | async-start | bytes 32768 | tf_op jit(solution)/shard_map/all_to_all | solution.py:65
  98.6 16.3 %all-to-all-start.7 = ((f32[32,2,1024]{2,1,0:T(2,128)}), f32[32,2,1024]{2,1,0:T(2,128)S(1)}, u32[]{:S(2)}, u32[]{:S(2)}) async-start(f32[32,2,1024]{2,1,0:T(2,128)} %copy.43), calls=%async_computation.7 | async-start | bytes 524288 | tf_op jit(solution)/shard_map/all_to_all | solution.py:58
where the time goes:
time: 118 us; the launch traced here: 117 us
  starting transfers between devices  36.1 us (31%)
  waiting for transfers between devices  32.5 us (28%)
  matrix products  19.7 us (17%)
  other arithmetic  15.3 us (13%)
  local copies, waits for them, and re-layouts  13.1 us (11%)
    all_to_all x4, waiting for transfers between devices, shards(): lax.all_to_all(outgoing.reshape(owners, CAP, flat_width), ('gx', 'gy', 'g...  31.1 us
    all_to_all x4, starting transfers between devices, shards(): lax.all_to_all(outgoing.reshape(owners, CAP, flat_width), ('gx', 'gy', 'g...  21.9 us
    all_to_all x4, starting transfers between devices, shards(): lax.all_to_all(labels.reshape(owners, CAP), ('gx', 'gy', 'gz'), split_axi...  14.2 us
    dot_general x5, matrix products, shards(): jnp.einsum('srb,sbc->src', work_rows, diag_inverse[level_at], preferred_e...  6.84 us
    dot_general x4, matrix products, shards(): jnp.einsum('krb,kbc->krc', picked, off_blocks[level_at], preferred_elemen...  6.41 us
    lt x5, other arithmetic, shards(): slot_ids < live_counts[level_at, 0]  4.31 us
    dot_general x4, local copies, waits for them, and re-layouts, shards(): jnp.dot(packer.astype(jnp.float32), contribution, precision=lax.Precision...  3.58 us
    convert_element_type x4, other arithmetic, shards(): work_rows = (right_side[level_at] - pending).astype(jnp.bfloat16)  3.41 us
  transfers between devices with their start and end apart: 8, of which 5 were waited for; matrix products, arithmetic and copies ran while one was open for 34% of the time, Pallas kernels for 0%

commit v1 on v0

v1 whole, which is shorter than its diff:
```python
import functools

import jax
import jax.numpy as jnp
from jax import lax
from jax.experimental import pallas as pl
from jax.experimental.pallas import tpu as pltpu
from jax.sharding import PartitionSpec as P


CAP = 2
AXES = ("gx", "gy", "gz")
VMEM = pl.BlockSpec(memory_space=pltpu.VMEM)
SMEM = pl.BlockSpec(memory_space=pltpu.SMEM)
HBM = pl.BlockSpec(memory_space=pltpu.HBM)
PARAMS = pltpu.CompilerParams(vmem_limit_bytes=16 * 1024 * 1024)


def assign_places(target, taken, owners, store):
    for level in range(target.shape[0]):
        for owner in range(owners):
            taken[owner] = 0
        for record in range(target.shape[1]):
            owner = target[level, record]
            count = taken[owner]
            taken[owner] = count + 1
            store(level, record, owner * CAP + count)


def solve(live_count, work_of, diag, solved):
    for slot in range(solved.shape[0]):
        work = work_of(slot).astype(jnp.bfloat16)
        out = jnp.dot(work, diag[slot], preferred_element_type=jnp.float32)
        solved[slot] = jnp.where(slot < live_count, out, jnp.zeros_like(out))


def first_kernel(owners, slots, *refs):
    live, source, target, owner_rows, block_rows, rhs, diag, off = refs[:8]
    answer, outgoing, token, rhs_now, diag_now, off_now, solved, taken, place, sems = refs[8:]
    load_rhs = pltpu.make_async_copy(rhs.at[0], rhs_now, sems.at[0])
    load_diag = pltpu.make_async_copy(diag.at[0], diag_now, sems.at[1])
    load_off = pltpu.make_async_copy(off.at[0], off_now, sems.at[2])
    load_rhs.start()
    load_diag.start()
    load_off.start()
    token[0] = 0
    steps, records = owner_rows.shape
    rows, width = solved.shape[1:]
    chunk = CAP * rows + 1
    out = outgoing.reshape(owners * chunk, width)

    def keep(level, record, where):
        place[record] = (where // CAP) * chunk + (where % CAP) * rows

    assign_places(target.at[pl.ds(0, 1)], taken, owners, keep)
    blocks = (steps + 1) * slots
    base = 1 << blocks.bit_length()
    none = jnp.float32(records * base)
    ids = lax.broadcasted_iota(jnp.int32, (owners, records), 0)
    order = lax.broadcasted_iota(jnp.int32, (owners, records), 1) * base
    lane = lax.broadcasted_iota(jnp.int32, (owners, width), 1)
    labels = jnp.zeros((owners, width), jnp.float32)
    for level in range(steps):
        hit = owner_rows[level : level + 1, :] == ids
        coded = (order + block_rows[level : level + 1, :]).astype(jnp.float32)
        low = jnp.min(jnp.where(hit, coded, none), axis=1, keepdims=True)
        high = jnp.max(jnp.where(hit, coded, jnp.float32(-1)), axis=1, keepdims=True)
        for at, value in enumerate((low, high)):
            label = (value.astype(jnp.int32) & (base - 1)).astype(jnp.float32)
            label = jnp.where(low < none, label, jnp.float32(blocks))
            labels = jnp.where(lane == level * CAP + at, label, labels)
    for owner in range(owners):
        out[owner * chunk + CAP * rows : (owner + 1) * chunk, :] = labels[owner : owner + 1, :]
    load_rhs.wait()
    load_diag.wait()
    solve(live[0], lambda slot: rhs_now[slot], diag_now, solved)
    store = pltpu.make_async_copy(solved, answer.at[0], sems.at[3])
    store.start()
    load_off.wait()
    for record in range(records):
        picked = solved[source[0, record]].astype(jnp.bfloat16)
        value = jnp.dot(picked, off_now[record], preferred_element_type=jnp.float32)
        out[pl.ds(place[record], rows), :] = value
    store.wait()


def fetch_kernel(owners, token, live, source, target, rhs, diag, off, *refs):
    live_now, source_now, place_now, rhs_now, diag_now, diag_next, off_now, taken, sems = refs
    loads = (
        (live, live_now),
        (source, source_now),
        (rhs.at[1], rhs_now),
        (diag.at[1], diag_now),
        (off.at[1], off_now),
        (diag.at[2], diag_next),
    )
    copies = [pltpu.make_async_copy(x, y, sems.at[at]) for at, (x, y) in enumerate(loads)]
    for copy in copies:
        copy.start()

    def keep(level, record, where):
        place_now[level, record] = where

    assign_places(target, taken, owners, keep)
    for copy in copies:
        copy.wait()


def later_kernel(level, levels, owners, *refs):
    last = level == levels - 1
    refs = list(refs)
    live, rhs, diag, arrived = refs[:4]
    refs = refs[4:]
    labels = refs.pop(0) if level > 1 else None
    if not last:
        source, place, off = refs[:3]
        refs = refs[3:]
        rhs_all = refs.pop(0)
        diag_all, off_all = (refs.pop(0), refs.pop(0)) if level < levels - 2 else (None, None)
    before = refs.pop(0) if level > 1 else None
    refs.pop(0)
    answer = refs.pop(0)
    if not last:
        outgoing, after, rhs_near = refs[:3]
        refs = refs[3:]
        diag_near, off_near = (refs.pop(0), refs.pop(0)) if diag_all is not None else (None, None)
    if level == 1:
        labels = refs.pop(0)
    solved, total, sems = refs[:3]
    sem = sems.at[0]
    ahead = []
    if not last:
        ahead.append(pltpu.make_async_copy(rhs_all.at[level + 1], rhs_near, sems.at[1]))
        if diag_all is not None:
            ahead.append(pltpu.make_async_copy(off_all.at[level + 1], off_near, sems.at[2]))
            ahead.append(pltpu.make_async_copy(diag_all.at[level + 2], diag_near, sems.at[3]))
    for copy in ahead:
        copy.start()
    slots, rows, width = solved.shape
    left = levels - level
    chunk = CAP * rows
    if level == 1:
        gathered, turned = refs[3:]
        flat = arrived.reshape(arrived.shape[0], width)
        for owner in range(owners):
            at = owner * (chunk + 1) + chunk
            gathered[owner : owner + 1, :] = flat[at : at + 1, :]
        turned[...] = gathered[...].T[: turned.shape[0], :].astype(jnp.int32)
        copy = pltpu.make_async_copy(turned, labels, sem)
        copy.start()
        total[...] = jnp.zeros_like(total)
        copy.wait()
    else:
        total[0 : left * slots] = before[...]
    for owner in range(owners):
        for at in range(CAP):
            label = labels[(level - 1) * CAP + at, owner] - level * slots
            if level == 1:
                start = owner * (chunk + 1) + at * rows
                value = flat[start : start + rows, :]
            else:
                value = arrived[owner * CAP + at]
            total[label] += value
    solve(live[level], lambda slot: rhs[slot] - total[slot], diag, solved)
    store = pltpu.make_async_copy(solved, answer.at[level], sem)
    store.start()
    if not last:
        for record in range(off.shape[0]):
            picked = solved[source[level, record]].astype(jnp.bfloat16)
            value = jnp.dot(picked, off[record], preferred_element_type=jnp.float32)
            outgoing[place[level, record]] = value
        after[...] = total[slots : left * slots]
    store.wait()
    for copy in ahead:
        copy.wait()


def shards(right_side, diag_inverse, off_blocks, live_counts, source_slot, target_owner, target_block):
    levels, slots, rows, width = right_side.shape
    records = off_blocks.shape[1]
    owners = lax.axis_size(AXES)
    steps = levels - 1
    chunk = CAP * rows
    f32, bf16, i32 = jnp.float32, jnp.bfloat16, jnp.int32
    near, table, semaphores = pltpu.VMEM, pltpu.SMEM, pltpu.SemaphoreType.DMA
    in_hbm = functools.partial(pltpu.with_memory_space_constraint, memory_space=pltpu.HBM)
    live, source, target, rhs, diag, off = (
        in_hbm(x)
        for x in (live_counts.reshape(levels), source_slot, target_owner, right_side, diag_inverse, off_blocks)
    )

    def exchange(parts):
        return lax.all_to_all(parts, AXES, split_axis=0, concat_axis=0, tiled=True)

    answer, outgoing, token = pl.pallas_call(
        functools.partial(first_kernel, owners, slots),
        out_shape=[
            pltpu.HBM((levels, slots, rows, width), f32),
            near((owners * (chunk + 1), 1, width), f32),
            table((1,), i32),
        ],
        in_specs=[SMEM] * 3 + [VMEM] * 2 + [HBM] * 3,
        out_specs=[HBM, VMEM, SMEM],
        scratch_shapes=[
            near((slots, rows, width), f32),
            near((slots, width, width), bf16),
            near((records, width, width), bf16),
            near((slots, rows, width), f32),
            table((owners,), i32),
            table((records,), i32),
            semaphores((4,)),
        ],
        name="level_0",
        compiler_params=PARAMS,
    )(live, source, target, target, in_hbm(target_block), rhs, diag, off)
    arrived = exchange(outgoing.reshape(owners, chunk + 1, 1, width))
    arrived = arrived.reshape(owners * (chunk + 1), 1, width)

    live, source, place, rhs_now, diag_now, diag_next, off_now = pl.pallas_call(
        functools.partial(fetch_kernel, owners),
        out_shape=[
            table((levels,), i32),
            table((steps, records), i32),
            table((steps, records), i32),
            near((slots, rows, width), f32),
            near((slots, width, width), bf16),
            near((slots, width, width), bf16),
            near((records, width, width), bf16),
        ],
        in_specs=[SMEM, HBM, HBM, SMEM] + [HBM] * 3,
        out_specs=[SMEM] * 3 + [VMEM] * 4,
        scratch_shapes=[table((owners,), i32), semaphores((6,))],
        name="fetch",
        compiler_params=PARAMS,
    )(token, live, source, target, rhs, diag, off)

    labels = before = None
    for level in range(1, levels):
        last = level == levels - 1
        left = levels - level
        operands = [(live, SMEM), (rhs_now, VMEM), (diag_now, VMEM), (arrived, VMEM)]
        if level > 1:
            operands.append((labels, SMEM))
        if not last:
            operands += [(source, SMEM), (place, SMEM), (off_now, VMEM), (rhs, HBM)]
            if level < steps - 1:
                operands += [(diag, HBM), (off, HBM)]
        if level > 1:
            operands.append((before, VMEM))
        operands.append((in_hbm(answer), HBM))
        outs = [(pltpu.HBM((levels, slots, rows, width), f32), HBM)]
        scratch = [near((slots, rows, width), f32), near((left * slots + 1, rows, width), f32)]
        scratch.append(semaphores((4,)))
        if not last:
            outs.append((near((owners * CAP, rows, width), f32), VMEM))
            outs.append((near(((left - 1) * slots, rows, width), f32), VMEM))
            outs.append((near((slots, rows, width), f32), VMEM))
            if level < steps - 1:
                outs.append((near((slots, width, width), bf16), VMEM))
                outs.append((near((records, width, width), bf16), VMEM))
        if level == 1:
            outs.append((table((steps * CAP, owners), i32), SMEM))
            scratch += [near((owners, width), f32), near((steps * CAP, owners), i32)]
        made = pl.pallas_call(
            functools.partial(later_kernel, level, levels, owners),
            out_shape=[shape for shape, _ in outs],
            in_specs=[spec for _, spec in operands],
            out_specs=[spec for _, spec in outs],
            input_output_aliases={len(operands) - 1: 0},
            scratch_shapes=scratch,
            compiler_params=PARAMS,
        )(*[value for value, _ in operands])
        answer = made[0]
        if last:
            return answer
        before, rhs_now = made[2:4]
        diag_now = diag_next
        if level < steps - 1:
            diag_next, off_now = made[4:6]
        if level == 1:
            labels = made[-1]
        arrived = exchange(made[1].reshape(owners, chunk, width))
        arrived = arrived.reshape(owners * CAP, rows, width)


def solution(mesh):
    spread = P(None, AXES)
    return jax.shard_map(
        shards,
        mesh=mesh,
        in_specs=(P(None, AXES, None, None),) * 3 + (spread,) * 4,
        out_specs=P(None, AXES, None, None),
        check_vma=False,
    )
```

time: 118 us -> 67.2 us (0.57)
  blocking collectives: 0 us -> 38 us
  starting transfers between devices: 36.1 us -> 7.09 us
  waiting for transfers between devices: 32.5 us -> 8.52 us
  matrix products: 19.7 us -> 0 us
  other arithmetic: 15.3 us -> 0 us
  Pallas kernels: 0 us -> 13.1 us
  local copies, waits for them, and re-layouts: 13.1 us -> 0 us
    all_to_all x0 -> x3, blocking collectives: none -> 38 us  [exchange(): return lax.all_to_all(parts, AXES, split_axis=0, concat_axis=0, tiled=True)]
    all_to_all x8 -> x1, starting transfers between devices: 36.1 us -> 7.09 us  [exchange(): return lax.all_to_all(parts, AXES, split_axis=0, concat_axis=0, tiled=True)]
    all_to_all x8 -> x1, waiting for transfers between devices: 32.5 us -> 8.52 us  [exchange(): return lax.all_to_all(parts, AXES, split_axis=0, concat_axis=0, tiled=True)]
    dot_general x21 -> x0, matrix products: 19.7 us -> none  [the longest x5 6.84 us: shards(): jnp.einsum('srb,sbc->src', work_rows, diag_inverse[level_at], preferred_e...]
    pallas_call x0 -> x6, Pallas kernels: none -> 13.1 us  [the longest x4 7.35 us: shards(): pl.pallas_call(functools.partial(later_kernel, level, levels, owners), ou...]
    lt x5 -> x0, other arithmetic: 4.31 us -> none  [shards(): slot_ids < live_counts[level_at, 0]]
    convert_element_type x8 -> x0, other arithmetic: 3.7 us -> none  [the longest x4 3.41 us: shards(): work_rows = (right_side[level_at] - pending).astype(jnp.bfloat16)]
    eq x6 -> x0, local copies, waits for them, and re-layouts: 3.66 us -> none  [the longest x4 1.55 us: shards(): block_ids[:, None] == received_labels[None, :]]
  transfers between devices with their start and end apart: 8 -> 1, of which waited for: 5 -> 1; matrix products, arithmetic and copies ran while one was open for 34% -> 0% of each run, Pallas kernels for 0% -> 3%
where the time goes in v1:
time: 67.2 us; the launch traced here: 66.8 us
  blocking collectives  38 us (57%)
  Pallas kernels  13.1 us (19%)
  waiting for transfers between devices  8.52 us (13%)
  starting transfers between devices  7.09 us (11%)
    all_to_all x3, blocking collectives, exchange(): return lax.all_to_all(parts, AXES, split_axis=0, concat_axis=0, tiled=True)  38 us
    all_to_all x1, waiting for transfers between devices, exchange(): return lax.all_to_all(parts, AXES, split_axis=0, concat_axis=0, tiled=True)  8.52 us
    pallas_call x4, Pallas kernels, shards(): pl.pallas_call(functools.partial(later_kernel, level, levels, owners), ou...  7.35 us
    all_to_all x1, starting transfers between devices, exchange(): return lax.all_to_all(parts, AXES, split_axis=0, concat_axis=0, tiled=True)  7.09 us
    pallas_call x1, Pallas kernels, shards(): pl.pallas_call(functools.partial(first_kernel, owners, slots), out_shape=...  3.47 us
    pallas_call x1, Pallas kernels, shards(): pl.pallas_call(functools.partial(fetch_kernel, owners), out_shape=[table(...  2.3 us
  transfers between devices with their start and end apart: 1, of which 1 were waited for; matrix products, arithmetic and copies ran while one was open for 0% of the time, Pallas kernels for 3%

profile of v1, /device:TPU:1, one launch (start us, length us, event | category | flops | bytes accessed | tf_op | source)
XLA Modules:
  0.0 66.8 jit_solution(6413431811192644181)
XLA Ops:
  0.0 3.5 %level_0.1 = (f32[5,16,8,128]{3,2,1,0:T(8,128)}, f32[544,1,128]{2,1,0:T(1,128)}, s32[1]{0:T(128)S(4)}) custom-call(s32[5]{0:T(128)} %bitcast.16, s32[4,32]{1,0:T(4,128)} %source.1, s32[4,32]{1,0:T(4,128)} %target.1, s32[4,32]{1,0:T(4,128)} %target.1, s32[4,32]{1,0:T(4,128)} %refs_4_.1, f32[5,16,8,128]{3,2,1,0:T(8,128)} %refs_8_.5, ...), custom_call_target="tpu_custom_call" | custom-call | tf_op jit(solution)/shard_map/level_0/pallas_call | solution.py:195
  3.5 7.1 %all-to-all-start = ((f32[32,17,1,128]{3,2,1,0:T(1,128)}), f32[32,17,1,128]{3,2,1,0:T(1,128)S(1)}, u32[]{:S(2)}, u32[]{:S(2)}) async-start(f32[32,17,1,128]{3,2,1,0:T(1,128)} %bitcast.1), calls=%async_computation | async-start | bytes 557056 | tf_op jit(solution)/shard_map/all_to_all | solution.py:193
  10.6 2.3 %fetch.1 = (s32[5]{0:T(128)S(4)}, s32[4,32]{1,0:T(4,128)S(4)}, s32[4,32]{1,0:T(4,128)S(4)}, f32[16,8,128]{2,1,0:T(8,128)S(1)}, bf16[16,128,128]{2,1,0:T(8,128)(2...) custom-call(s32[1]{0:T(128)S(4)} %get-tuple-element.32.token, s32[5]{0:T(128)} %bitcast.17, ...), custom_call_target="tpu_custom_call" | custom-call | tf_op jit(solution)/shard_map/fetch/pallas_call | solution.py:219
  12.9 8.5 %all-to-all-done = f32[32,17,1,128]{3,2,1,0:T(1,128)S(1)} async-done(((f32[32,17,1,128]{3,2,1,0:T(1,128)}), f32[32,17,1,128]{3,2,1,0:T(1,128)S(1)}, u32[]{:S(2)}, u32[]{:S(2)}) %all-to-all-start) | async-done | bytes 278560 | tf_op jit(solution)/shard_map/all_to_all | solution.py:193
  21.4 2.2 %shard_map.73 = (f32[5,16,8,128]{3,2,1,0:T(8,128)}, f32[64,8,128]{2,1,0:T(8,128)S(1)}, f32[48,8,128]{2,1,0:T(8,128)S(1)}, f32[16,8,128]{2,1,0:T(8,128)S(1)}, bf1...) custom-call(s32[5]{0:T(128)S(4)} %get-tuple-element.33.refs_0_, ...), custom_call_target="tpu_custom_call", output_to_operand_aliasing={{0}: (10, {})} | custom-call | tf_op jit(solution)/shard_map/pallas_call | solution.py:264
  23.6 12.7 %all_to_all.20 = f32[32,16,128]{2,1,0:T(8,128)S(1)} all-to-all(f32[32,16,128]{2,1,0:T(8,128)S(1)} %bitcast.13), channel_id=1, replica_groups=mesh['gx'=4,'gy'=4,'gz'=2] {'gx','gy','gz'}, dimensions={0} | all-to-all | bytes 524288 | tf_op jit(solution)/shard_map/all_to_all | solution.py:193
  36.3 2.3 %shard_map.74 = (f32[5,16,8,128]{3,2,1,0:T(8,128)}, f32[64,8,128]{2,1,0:T(8,128)S(1)}, f32[32,8,128]{2,1,0:T(8,128)S(1)}, f32[16,8,128]{2,1,0:T(8,128)S(1)}, bf1...) custom-call(s32[5]{0:T(128)S(4)} %get-tuple-element.33.refs_0_, ...), custom_call_target="tpu_custom_call", output_to_operand_aliasing={{0}: (12, {})} | custom-call | tf_op jit(solution)/shard_map/pallas_call | solution.py:264
  38.6 12.7 %all_to_all.21 = f32[32,16,128]{2,1,0:T(8,128)S(1)} all-to-all(f32[32,16,128]{2,1,0:T(8,128)S(1)} %bitcast.14), channel_id=1, replica_groups=mesh['gx'=4,'gy'=4,'gz'=2] {'gx','gy','gz'}, dimensions={0} | all-to-all | bytes 524288 | tf_op jit(solution)/shard_map/all_to_all | solution.py:193
  51.3 1.7 %shard_map.75 = (f32[5,16,8,128]{3,2,1,0:T(8,128)}, f32[64,8,128]{2,1,0:T(8,128)S(1)}, f32[16,8,128]{2,1,0:T(8,128)S(1)}, f32[16,8,128]{2,1,0:T(8,128)S(1)}) custom-call(s32[5]{0:T(128)S(4)} %get-tuple-element.33.refs_0_, f32[16,8,128]{2,1,0:T(8,128)S(1)} %get-tuple-element.48.refs_1_, ...), custom_call_target="tpu_custom_call", output_to_operand_aliasing={{0}: (10, {})} | custom-call | tf_op jit(solution)/shard_map/pallas_call | solution.py:264
  53.0 12.6 %all_to_all.22 = f32[32,16,128]{2,1,0:T(8,128)S(1)} all-to-all(f32[32,16,128]{2,1,0:T(8,128)S(1)} %bitcast.15), channel_id=1, replica_groups=mesh['gx'=4,'gy'=4,'gz'=2] {'gx','gy','gz'}, dimensions={0} | all-to-all | bytes 524288 | tf_op jit(solution)/shard_map/all_to_all | solution.py:193
  65.6 1.2 %shard_map.76 = f32[5,16,8,128]{3,2,1,0:T(8,128)} custom-call(s32[5]{0:T(128)S(4)} %get-tuple-element.33.refs_0_, f32[16,8,128]{2,1,0:T(8,128)S(1)} %get-tuple-element.54.refs_1_, bf16[16,128,128]{2,1,0:T(8,128)(2,1)S(1)} %get-tuple-element.55.refs_2_, f32[64,8,128]{2,1,0:T(8,128)S(1)} %bitcast.12, ...), custom_call_target="tpu_custom_call", output_to_operand_aliasing={{}: (6, {})} | custom-call | tf_op jit(solution)/shard_map/pallas_call | solution.py:264
Async XLA Ops:
  3.5 17.9 %all-to-all-start = ((f32[32,17,1,128]{3,2,1,0:T(1,128)}), f32[32,17,1,128]{3,2,1,0:T(1,128)S(1)}, u32[]{:S(2)}, u32[]{:S(2)}) async-start(f32[32,17,1,128]{3,2,1,0:T(1,128)} %bitcast.1), calls=%async_computation | async-start | bytes 557056 | tf_op jit(solution)/shard_map/all_to_all | solution.py:193

commit v2 on v0

v2 whole, which is shorter than its diff:
```python
import functools

import jax
import jax.numpy as jnp
from jax import lax
from jax.experimental import pallas as pl
from jax.experimental.pallas import tpu as pltpu
from jax.sharding import PartitionSpec as P

CAP = 2
AXES = ("gx", "gy", "gz")
VMEM = pl.BlockSpec(memory_space=pltpu.VMEM)
SMEM = pl.BlockSpec(memory_space=pltpu.SMEM)
HBM = pl.BlockSpec(memory_space=pltpu.HBM)
PARAMS = pltpu.CompilerParams(vmem_limit_bytes=16 * 1024 * 1024)
PIECES = 4


class Copies:
    def __init__(self, sems):
        self.sems, self.used = sems, 0

    def start(self, source, target):
        copy = pltpu.make_async_copy(source, target, self.sems.at[self.used])
        self.used += 1
        copy.start()
        return copy


def wait(*copies):
    for copy in copies:
        copy.wait()


def pieces(count):
    size = -(-count // (2 * PIECES)) * 2
    return [(at, min(size, count - at)) for at in range(0, count, size)]


def products(left, blocks, start, count):
    found = []
    rows, width = left(0).shape
    none = jnp.zeros((rows, width), jnp.float32)
    for at in range(0, count - 1, 2):
        upper = jnp.concatenate([left(at), none], axis=0).astype(jnp.bfloat16)
        lower = jnp.concatenate([none, left(at + 1)], axis=0).astype(jnp.bfloat16)
        pair = blocks[start + at : start + at + 2].reshape(2 * width, width)
        both = jnp.dot(jnp.concatenate([upper, lower], axis=1), pair, preferred_element_type=jnp.float32)
        found += [both[:rows], both[rows:]]
    if count % 2:
        one = left(count - 1).astype(jnp.bfloat16)
        found.append(jnp.dot(one, blocks[start + count - 1], preferred_element_type=jnp.float32))
    return found


def solve(live_count, work_of, diag, solved):
    for slot, out in enumerate(products(work_of, diag, 0, solved.shape[0])):
        solved[slot] = jnp.where(slot < live_count, out, jnp.zeros_like(out))


def first_kernel(owners, *refs):
    live, source, target, block, rhs, diag, off = refs[:7]
    outgoing, solved, live_now, source_now, place = refs[7:12]
    target_now, owner_rows, block_rows, taken, rhs_now, diag_now, off_now, sems = refs[12:]
    copies = Copies(sems)
    tables = [
        copies.start(target, target_now),
        copies.start(target, owner_rows),
        copies.start(block, block_rows),
        copies.start(source, source_now),
        copies.start(live, live_now),
    ]
    load_rhs = copies.start(rhs.at[0], rhs_now)
    load_diag = copies.start(diag.at[0], diag_now)
    steps, records = owner_rows.shape
    slots, rows, width = solved.shape
    chunk = CAP * rows + 1
    out = outgoing.reshape(owners * chunk, width)
    parts = pieces(records)
    load_off = [copies.start(off.at[0, pl.ds(at, size)], off_now.at[pl.ds(at, size)]) for at, size in parts]
    wait(*tables)

    for level in range(steps):
        for owner in range(owners):
            taken[level, owner] = 0
    for record in range(records):
        for level in range(steps):
            owner = target_now[level, record]
            count = taken[level, owner]
            taken[level, owner] = count + 1
            if level == 0:
                place[level, record] = owner * chunk + count * rows
            else:
                place[level, record] = owner * CAP + count

    blocks = (steps + 1) * slots
    base = 1 << blocks.bit_length()
    none = jnp.float32(records * base)
    ids = lax.broadcasted_iota(jnp.int32, (owners, records), 0)
    order = lax.broadcasted_iota(jnp.int32, (owners, records), 1) * base
    lane = lax.broadcasted_iota(jnp.int32, (owners, width), 1)
    labels = jnp.zeros((owners, width), jnp.float32)
    for level in range(steps):
        hit = owner_rows[level : level + 1, :] == ids
        coded = (order + block_rows[level : level + 1, :]).astype(jnp.float32)
        low = jnp.min(jnp.where(hit, coded, none), axis=1, keepdims=True)
        high = jnp.max(jnp.where(hit, coded, jnp.float32(-1)), axis=1, keepdims=True)
        for at, value in enumerate((low, high)):
            label = (value.astype(jnp.int32) & (base - 1)).astype(jnp.float32)
            label = jnp.where(low < none, label, jnp.float32(blocks))
            labels = jnp.where(lane == level * CAP + at, label, labels)
    for owner in range(owners):
        out[owner * chunk + CAP * rows : (owner + 1) * chunk, :] = labels[owner : owner + 1, :]

    wait(load_rhs, load_diag)
    solve(live_now[0], lambda slot: rhs_now[slot], diag_now, solved)
    for (at, size), copy in zip(parts, load_off):
        copy.wait()
        values = products(lambda i: solved[source_now[0, at + i]], off_now, at, size)
        for record, value in enumerate(values, at):
            out[pl.ds(place[0, record], rows), :] = value


def work_of_level(level, levels, owners, at, copies):
    solved, labels, live = at["solved"], at["labels"], at["live"]
    slots, rows, width = solved.shape
    last = level == levels - 1
    left = levels - level
    chunk = CAP * rows
    totals = at["even"], at["odd"]
    if level == 1:
        gathered, turned = at["gathered"], at["turned"]
        flat = at["arrived"].reshape(owners * (chunk + 1), width)
        for owner in range(owners):
            row = owner * (chunk + 1) + chunk
            gathered[owner : owner + 1, :] = flat[row : row + 1, :]
        turned[...] = gathered[...].T[: turned.shape[0], :].astype(jnp.int32)
        copy = copies.start(turned, labels)
        totals[0][...] = jnp.zeros_like(totals[0])
        totals[1][...] = jnp.zeros_like(totals[1])
        copy.wait()
    else:
        totals[0][0 : left * slots] = at["before"][...]
        totals[1][...] = jnp.zeros_like(totals[1])
    for owner in range(owners):
        for which, total in enumerate(totals):
            label = labels[(level - 1) * CAP + which, owner] - level * slots
            if level == 1:
                start = owner * (chunk + 1) + which * rows
                value = flat[start : start + rows, :]
            else:
                value = at["arrived"][owner * CAP + which]
            total[label] += value
    rhs = at["rhs"].at[level]
    solve(live[level], lambda slot: rhs[slot] - (totals[0][slot] + totals[1][slot]), at["diag"].at[level], solved)
    if last:
        wait(copies.start(solved, at["answer"].at[level]))
    else:
        off = at["off"].at[level]
        values = products(lambda i: solved[at["source"][level, i]], off, 0, off.shape[0])
        for record, value in enumerate(values):
            at["outgoing"][at["place"][level, record]] = value
        at["after"][...] = totals[0][slots : left * slots] + totals[1][slots : left * slots]


def later_kernel(level, levels, owners, names, *refs):
    at = dict(zip(names, refs))
    last = level == levels - 1
    copies = Copies(at["sems"])
    live = at["live"]
    ahead = [copies.start(at["solved_before"], at["answer"].at[level - 1])]

    @pl.when(live[level] >= 0)
    def _():
        work_of_level(level, levels, owners, at, copies)

    wait(*ahead)


def shards(right_side, diag_inverse, off_blocks, live_counts, source_slot, target_owner, target_block):
    levels, slots, rows, width = right_side.shape
    records = off_blocks.shape[1]
    owners = lax.axis_size(AXES)
    steps = levels - 1
    chunk = CAP * rows
    f32, bf16, i32 = jnp.float32, jnp.bfloat16, jnp.int32
    near, table, semaphores = pltpu.VMEM, pltpu.SMEM, pltpu.SemaphoreType.DMA
    rows_shape = (slots, rows, width)
    diag_shape, off_shape = (slots, width, width), (records, width, width)
    arguments = (live_counts.reshape(levels), source_slot, target_owner, target_block)
    arguments += (right_side, diag_inverse, off_blocks)
    arguments = [pltpu.with_memory_space_constraint(x, pltpu.HBM) for x in arguments]
    rhs, diag, off = (
        pltpu.with_memory_space_constraint(x, pltpu.VMEM) for x in (right_side, diag_inverse, off_blocks)
    )

    def exchange(parts):
        return lax.all_to_all(parts, AXES, split_axis=0, concat_axis=0, tiled=True)

    outgoing, solved, live, source, place = pl.pallas_call(
        functools.partial(first_kernel, owners),
        out_shape=[
            near((owners * (chunk + 1), 1, width), f32),
            near(rows_shape, f32),
            table((levels,), i32),
            table((steps, records), i32),
            table((steps, records), i32),
        ],
        in_specs=[HBM] * 7,
        out_specs=[VMEM, VMEM, SMEM, SMEM, SMEM],
        scratch_shapes=[
            table((steps, records), i32),
            near((steps, records), i32),
            near((steps, records), i32),
            table((steps, owners), i32),
            near(rows_shape, f32),
            near(diag_shape, bf16),
            near(off_shape, bf16),
            semaphores((11 + PIECES,)),
        ],
        name="level_0",
        compiler_params=PARAMS,
    )(*arguments)
    arrived = exchange(outgoing.reshape(owners, chunk + 1, 1, width)).reshape(owners * (chunk + 1), 1, width)

    answer = labels = before = None
    for level in range(1, levels):
        last = level == levels - 1
        left = levels - level
        ins = [("live", live, SMEM), ("rhs", rhs, VMEM), ("diag", diag, VMEM), ("arrived", arrived, VMEM)]
        ins.append(("solved_before", solved, VMEM))
        outs = [("answer", pltpu.HBM((levels, *rows_shape), f32), HBM)]
        scratch = [("even", near((left * slots + 1, rows, width), f32)), ("odd", near((left * slots + 1, rows, width), f32))]
        scratch.append(("sems", semaphores((6,))))
        if level == 1:
            outs.append(("labels", table((steps * CAP, owners), i32), SMEM))
            scratch += [("gathered", near((owners, width), f32)), ("turned", near((steps * CAP, owners), i32))]
        else:
            ins += [("labels", labels, SMEM), ("before", before, VMEM)]
        if last:
            scratch.append(("solved", near(rows_shape, f32)))
        else:
            ins += [("source", source, SMEM), ("place", place, SMEM), ("off", off, VMEM)]
            outs.append(("solved", near(rows_shape, f32), VMEM))
            outs.append(("outgoing", near((owners * CAP, rows, width), f32), VMEM))
            outs.append(("after", near(((left - 1) * slots, rows, width), f32), VMEM))
        if level > 1:
            ins.append(("answer_before", pltpu.with_memory_space_constraint(answer, pltpu.HBM), HBM))
        names = [name for name, *_ in ins + outs + scratch]
        made = pl.pallas_call(
            functools.partial(later_kernel, level, levels, owners, names),
            out_shape=[shape for _, shape, _ in outs],
            in_specs=[spec for *_, spec in ins],
            out_specs=[spec for *_, spec in outs],
            input_output_aliases={len(ins) - 1: 0} if level > 1 else {},
            scratch_shapes=[shape for _, shape in scratch],
            name=f"level_{level}",
            compiler_params=PARAMS,
        )(*[value for _, value, _ in ins])
        made = dict(zip([name for name, *_ in outs], made))
        answer = made["answer"]
        if last:
            return answer
        solved, before = made["solved"], made["after"]
        labels = made.get("labels", labels)
        arrived = exchange(made["outgoing"].reshape(owners, chunk, width)).reshape(owners * CAP, rows, width)


def solution(mesh):
    spread = P(None, AXES)
    return jax.shard_map(
        shards,
        mesh=mesh,
        in_specs=(P(None, AXES, None, None),) * 3 + (spread,) * 4,
        out_specs=P(None, AXES, None, None),
        check_vma=False,
    )
```

time: 118 us -> 62.3 us (0.53)
  blocking collectives: 0 us -> 55.8 us
  starting transfers between devices: 36.1 us -> 0 us
  waiting for transfers between devices: 32.5 us -> 0 us
  matrix products: 19.7 us -> 0 us
  other arithmetic: 15.3 us -> 0 us
  local copies, waits for them, and re-layouts: 13.1 us -> 0.01 us
  Pallas kernels: 0 us -> 6.25 us
    all_to_all x0 -> x4, blocking collectives: none -> 55.8 us  [exchange(): return lax.all_to_all(parts, AXES, split_axis=0, concat_axis=0, tiled=True)]
    all_to_all x8 -> x0, starting transfers between devices: 36.1 us -> none  [the longest x4 21.9 us: shards(): lax.all_to_all(outgoing.reshape(owners, CAP, flat_width), ('gx', 'gy', 'g...]
    all_to_all x8 -> x0, waiting for transfers between devices: 32.5 us -> none  [the longest x4 31.1 us: shards(): lax.all_to_all(outgoing.reshape(owners, CAP, flat_width), ('gx', 'gy', 'g...]
    dot_general x21 -> x0, matrix products: 19.7 us -> none  [the longest x5 6.84 us: shards(): jnp.einsum('srb,sbc->src', work_rows, diag_inverse[level_at], preferred_e...]
    pallas_call x0 -> x5, Pallas kernels: none -> 6.25 us  [the longest x4 3.77 us: shards(): pl.pallas_call(functools.partial(later_kernel, level, levels, owners, nam...]
    lt x5 -> x0, other arithmetic: 4.31 us -> none  [shards(): slot_ids < live_counts[level_at, 0]]
    convert_element_type x8 -> x0, other arithmetic: 3.7 us -> none  [the longest x4 3.41 us: shards(): work_rows = (right_side[level_at] - pending).astype(jnp.bfloat16)]
    eq x6 -> x0, local copies, waits for them, and re-layouts: 3.66 us -> none  [the longest x4 1.55 us: shards(): block_ids[:, None] == received_labels[None, :]]
  transfers between devices with their start and end apart: 8 -> 0, of which waited for: 5 -> 0; matrix products, arithmetic and copies ran while one was open for 34% -> 0% of each run, Pallas kernels for 0% -> 0%
where the time goes in v2:
time: 62.3 us; the launch traced here: 62.1 us
  blocking collectives  55.8 us (90%)
  Pallas kernels  6.25 us (10%)
    all_to_all x4, blocking collectives, exchange(): return lax.all_to_all(parts, AXES, split_axis=0, concat_axis=0, tiled=True)  55.8 us
    pallas_call x4, Pallas kernels, shards(): pl.pallas_call(functools.partial(later_kernel, level, levels, owners, nam...  3.77 us
    pallas_call x1, Pallas kernels, shards(): pl.pallas_call(functools.partial(first_kernel, owners), out_shape=[near((...  2.48 us

profile of v2, /device:TPU:1, one launch (start us, length us, event | category | flops | bytes accessed | tf_op | source)
XLA Modules:
  0.0 62.1 jit_solution(9489584332661623085)
XLA Ops:
  0.0 0.0 copy-start.1
  0.0 0.0 copy-start.2
  0.0 0.0 copy-start
  0.0 2.5 %level_0.1 = (f32[544,1,128]{2,1,0:T(1,128)S(1)}, f32[16,8,128]{2,1,0:T(8,128)S(1)}, s32[5]{0:T(128)S(4)}, s32[4,32]{1,0:T(4,128)S(4)}, s32[4,32]{1,0:T(4,128)S(4)}) custom-call(s32[5]{0:T(128)} %bitcast.17, s32[4,32]{1,0:T(4,128)} %refs_1_.5, s32[4,32]{1,0:T(4,128)} %refs_2_.5, s32[4,32]{1,0:T(4,128)} %refs_3_.1, f32[5,16,8,128]{3,2,1,0:T(8,128)} %refs_1_.9, ...), custom_call_target="tpu_custom_call" | custom-call | tf_op jit(solution)/shard_map/level_0/pallas_call | solution.py:200
  2.5 17.7 %all_to_all.20 = f32[32,17,1,128]{3,2,1,0:T(1,128)S(1)} all-to-all(f32[32,17,1,128]{3,2,1,0:T(1,128)S(1)} %bitcast.13), channel_id=1, replica_groups=mesh['gx'=4,'gy'=4,'gz'=2] {'gx','gy','gz'}, dimensions={0} | all-to-all | bytes 557056 | tf_op jit(solution)/shard_map/all_to_all | solution.py:198
  20.2 0.0 copy-done.1
  20.2 0.0 copy-done.2
  20.2 0.0 copy-done
  20.2 1.3 %level_1.1 = (f32[5,16,8,128]{3,2,1,0:T(8,128)}, s32[8,32]{1,0:T(8,128)S(4)}, f32[16,8,128]{2,1,0:T(8,128)S(1)}, f32[64,8,128]{2,1,0:T(8,128)S(1)}, f32[48,8,128]{2,1,0:T(8,128)S(1)}) custom-call(s32[5]{0:T(128)S(4)} %get-tuple-element.23.refs_0_, f32[5,16,8,128]{3,2,1,0:T(8,128)S(1)} %copy-done.2, bf16[5,16,128,128]{3,2,1,0:T(8,128)(2,1)S(1)} %copy-done.1, ...), custom_call_target="tpu_custom_call" | custom-call | tf_op jit(solution)/shard_map/level_1/pallas_call | solution.py:250
  21.6 12.7 %all_to_all.21 = f32[32,16,128]{2,1,0:T(8,128)S(1)} all-to-all(f32[32,16,128]{2,1,0:T(8,128)S(1)} %bitcast.16), channel_id=1, replica_groups=mesh['gx'=4,'gy'=4,'gz'=2] {'gx','gy','gz'}, dimensions={0} | all-to-all | bytes 524288 | tf_op jit(solution)/shard_map/all_to_all | solution.py:198
  34.3 0.7 %level_2.1 = (f32[5,16,8,128]{3,2,1,0:T(8,128)}, f32[16,8,128]{2,1,0:T(8,128)S(1)}, f32[64,8,128]{2,1,0:T(8,128)S(1)}, f32[32,8,128]{2,1,0:T(8,128)S(1)}) custom-call(s32[5]{0:T(128)S(4)} %get-tuple-element.23.refs_0_, f32[5,16,8,128]{3,2,1,0:T(8,128)S(1)} %copy-done.2, bf16[5,16,128,128]{3,2,1,0:T(8,128)(2,1)S(1)} %copy-done.1, ...), custom_call_target="tpu_custom_call", output_to_operand_aliasing={{0}: (10, {})} | custom-call | tf_op jit(solution)/shard_map/level_2/pallas_call | solution.py:250
  35.0 12.7 %all_to_all.22 = f32[32,16,128]{2,1,0:T(8,128)S(1)} all-to-all(f32[32,16,128]{2,1,0:T(8,128)S(1)} %bitcast.15), channel_id=1, replica_groups=mesh['gx'=4,'gy'=4,'gz'=2] {'gx','gy','gz'}, dimensions={0} | all-to-all | bytes 524288 | tf_op jit(solution)/shard_map/all_to_all | solution.py:198
  47.6 0.7 %level_3.1 = (f32[5,16,8,128]{3,2,1,0:T(8,128)}, f32[16,8,128]{2,1,0:T(8,128)S(1)}, f32[64,8,128]{2,1,0:T(8,128)S(1)}, f32[16,8,128]{2,1,0:T(8,128)S(1)}) custom-call(s32[5]{0:T(128)S(4)} %get-tuple-element.23.refs_0_, f32[5,16,8,128]{3,2,1,0:T(8,128)S(1)} %copy-done.2, bf16[5,16,128,128]{3,2,1,0:T(8,128)(2,1)S(1)} %copy-done.1, ...), custom_call_target="tpu_custom_call", output_to_operand_aliasing={{0}: (10, {})} | custom-call | tf_op jit(solution)/shard_map/level_3/pallas_call | solution.py:250
  48.3 12.7 %all_to_all.23 = f32[32,16,128]{2,1,0:T(8,128)S(1)} all-to-all(f32[32,16,128]{2,1,0:T(8,128)S(1)} %bitcast.14), channel_id=1, replica_groups=mesh['gx'=4,'gy'=4,'gz'=2] {'gx','gy','gz'}, dimensions={0} | all-to-all | bytes 524288 | tf_op jit(solution)/shard_map/all_to_all | solution.py:198
  61.0 1.1 %level_4.1 = f32[5,16,8,128]{3,2,1,0:T(8,128)} custom-call(s32[5]{0:T(128)S(4)} %get-tuple-element.23.refs_0_, f32[5,16,8,128]{3,2,1,0:T(8,128)S(1)} %copy-done.2, bf16[5,16,128,128]{3,2,1,0:T(8,128)(2,1)S(1)} %copy-done.1, f32[64,8,128]{2,1,0:T(8,128)S(1)} %bitcast.12, f32[16,8,128]{2,1,0:T(8,128)S(1)} %get-tuple-element.38.refs_4_, ...), custom_call_target="tpu_custom_call", output_to_operand_aliasing={{}: (7, {})} | custom-call | tf_op jit(solution)/shard_map/level_4/pallas_call | solution.py:250
Async XLA Ops:
  0.0 20.2 %copy-start.1 = (bf16[5,16,128,128]{3,2,1,0:T(8,128)(2,1)S(1)}, bf16[5,16,128,128]{3,2,1,0:T(8,128)(2,1)}, u32[]{:S(2)}) copy-start(bf16[5,16,128,128]{3,2,1,0:T(8,128)(2,1)} %refs_2_.9) | copy-start | bytes 7864324
  0.0 20.2 %copy-start.2 = (f32[5,16,8,128]{3,2,1,0:T(8,128)S(1)}, f32[5,16,8,128]{3,2,1,0:T(8,128)}, u32[]{:S(2)}) copy-start(f32[5,16,8,128]{3,2,1,0:T(8,128)} %refs_1_.9) | copy-start | bytes 983044
  0.0 20.2 %copy-start = (bf16[4,32,128,128]{3,2,1,0:T(8,128)(2,1)S(1)}, bf16[4,32,128,128]{3,2,1,0:T(8,128)(2,1)}, u32[]{:S(2)}) copy-start(bf16[4,32,128,128]{3,2,1,0:T(8,128)(2,1)} %refs_9_.3) | copy-start | bytes 12582916

commit v3 on v2

--- a/solution.py
+++ b/solution.py
@@ -20,9 +20,12 @@
     def __init__(self, sems):
         self.sems, self.used = sems, 0
 
+    def make(self, source, target):
+        self.used += 1
+        return pltpu.make_async_copy(source, target, self.sems.at[self.used - 1])
+
     def start(self, source, target):
-        copy = pltpu.make_async_copy(source, target, self.sems.at[self.used])
-        self.used += 1
+        copy = self.make(source, target)
         copy.start()
         return copy
 
@@ -61,15 +64,10 @@
 def first_kernel(owners, *refs):
     live, source, target, block, rhs, diag, off = refs[:7]
     outgoing, solved, live_now, source_now, place = refs[7:12]
-    target_now, owner_rows, block_rows, taken, rhs_now, diag_now, off_now, sems = refs[12:]
+    owner_rows, block_rows, place_rows, rhs_now, diag_now, off_now, sems = refs[12:]
     copies = Copies(sems)
-    tables = [
-        copies.start(target, target_now),
-        copies.start(target, owner_rows),
-        copies.start(block, block_rows),
-        copies.start(source, source_now),
-        copies.start(live, live_now),
-    ]
+    tables = [copies.start(target, owner_rows), copies.start(block, block_rows)]
+    scalars = [copies.start(source, source_now), copies.start(live, live_now)]
     load_rhs = copies.start(rhs.at[0], rhs_now)
     load_diag = copies.start(diag.at[0], diag_now)
     steps, records = owner_rows.shape
@@ -79,19 +77,6 @@
     parts = pieces(records)
     load_off = [copies.start(off.at[0, pl.ds(at, size)], off_now.at[pl.ds(at, size)]) for at, size in parts]
     wait(*tables)
-
-    for level in range(steps):
-        for owner in range(owners):
-            taken[level, owner] = 0
-    for record in range(records):
-        for level in range(steps):
-            owner = target_now[level, record]
-            count = taken[level, owner]
-            taken[level, owner] = count + 1
-            if level == 0:
-                place[level, record] = owner * chunk + count * rows
-            else:
-                place[level, record] = owner * CAP + count
 
     blocks = (steps + 1) * slots
     base = 1 << blocks.bit_length()
@@ -105,15 +90,21 @@
         coded = (order + block_rows[level : level + 1, :]).astype(jnp.float32)
         low = jnp.min(jnp.where(hit, coded, none), axis=1, keepdims=True)
         high = jnp.max(jnp.where(hit, coded, jnp.float32(-1)), axis=1, keepdims=True)
+        is_first = jnp.where(hit & (coded == low), jnp.float32(1), jnp.float32(0))
+        second = 1 - jnp.sum(is_first, axis=0, keepdims=True).astype(jnp.int32)
+        owner_row = owner_rows[level : level + 1, :]
+        place_rows[level : level + 1, :] = owner_row * (CAP if level else chunk) + second * (1 if level else rows)
         for at, value in enumerate((low, high)):
             label = (value.astype(jnp.int32) & (base - 1)).astype(jnp.float32)
             label = jnp.where(low < none, label, jnp.float32(blocks))
             labels = jnp.where(lane == level * CAP + at, label, labels)
+    keep_place = copies.start(place_rows, place)
     for owner in range(owners):
         out[owner * chunk + CAP * rows : (owner + 1) * chunk, :] = labels[owner : owner + 1, :]
 
-    wait(load_rhs, load_diag)
+    wait(load_rhs, load_diag, *scalars)
     solve(live_now[0], lambda slot: rhs_now[slot], diag_now, solved)
+    keep_place.wait()
     for (at, size), copy in zip(parts, load_off):
         copy.wait()
         values = products(lambda i: solved[source_now[0, at + i]], off_now, at, size)
@@ -121,36 +112,48 @@
             out[pl.ds(place[0, record], rows), :] = value
 
 
-def work_of_level(level, levels, owners, at, copies):
-    solved, labels, live = at["solved"], at["labels"], at["live"]
-    slots, rows, width = solved.shape
-    last = level == levels - 1
+def add_arrived(level, levels, owners, at, keep_labels):
+    labels = at["labels"]
+    slots, rows, width = at["solved"].shape
     left = levels - level
     chunk = CAP * rows
     totals = at["even"], at["odd"]
     if level == 1:
-        gathered, turned = at["gathered"], at["turned"]
         flat = at["arrived"].reshape(owners * (chunk + 1), width)
-        for owner in range(owners):
-            row = owner * (chunk + 1) + chunk
-            gathered[owner : owner + 1, :] = flat[row : row + 1, :]
-        turned[...] = gathered[...].T[: turned.shape[0], :].astype(jnp.int32)
-        copy = copies.start(turned, labels)
         totals[0][...] = jnp.zeros_like(totals[0])
         totals[1][...] = jnp.zeros_like(totals[1])
-        copy.wait()
     else:
         totals[0][0 : left * slots] = at["before"][...]
         totals[1][...] = jnp.zeros_like(totals[1])
     for owner in range(owners):
+        if level == 1:
+            row = owner * (chunk + 1) + chunk
+            sent = flat[row : row + 1, :].astype(jnp.int32) - level * slots
         for which, total in enumerate(totals):
-            label = labels[(level - 1) * CAP + which, owner] - level * slots
+            if level == 1:
+                label = sent[0, which]
+            else:
+                label = labels[(level - 1) * CAP + which, owner] - level * slots
             if level == 1:
                 start = owner * (chunk + 1) + which * rows
                 value = flat[start : start + rows, :]
             else:
                 value = at["arrived"][owner * CAP + which]
             total[label] += value
+    if level == 1:
+        gathered, turned = at["gathered"], at["turned"]
+        for owner in range(owners):
+            row = owner * (chunk + 1) + chunk
+            gathered[owner : owner + 1, :] = flat[row : row + 1, :]
+        turned[...] = gathered[...].T[: turned.shape[0], :].astype(jnp.int32)
+        keep_labels.start()
+
+
+def solve_and_pack(level, levels, at, copies):
+    solved, live, totals = at["solved"], at["live"], (at["even"], at["odd"])
+    slots = solved.shape[0]
+    last = level == levels - 1
+    left = levels - level
     rhs = at["rhs"].at[level]
     solve(live[level], lambda slot: rhs[slot] - (totals[0][slot] + totals[1][slot]), at["diag"].at[level], solved)
     if last:
@@ -165,16 +168,21 @@
 
 def later_kernel(level, levels, owners, names, *refs):
     at = dict(zip(names, refs))
-    last = level == levels - 1
     copies = Copies(at["sems"])
     live = at["live"]
     ahead = [copies.start(at["solved_before"], at["answer"].at[level - 1])]
 
+    keep_labels = copies.make(at["turned"], at["labels"]) if level == 1 else None
+
     @pl.when(live[level] >= 0)
     def _():
-        work_of_level(level, levels, owners, at, copies)
-
-    wait(*ahead)
+        add_arrived(level, levels, owners, at, keep_labels)
+
+    @pl.when(live[level] >= 0)
+    def _():
+        solve_and_pack(level, levels, at, copies)
+
+    wait(*ahead, *([keep_labels] if level == 1 else []))
 
 
 def shards(right_side, diag_inverse, off_blocks, live_counts, source_slot, target_owner, target_block):
@@ -209,10 +217,9 @@
         in_specs=[HBM] * 7,
         out_specs=[VMEM, VMEM, SMEM, SMEM, SMEM],
         scratch_shapes=[
-            table((steps, records), i32),
             near((steps, records), i32),
             near((steps, records), i32),
-            table((steps, owners), i32),
+            near((steps, records), i32),
             near(rows_shape, f32),
             near(diag_shape, bf16),
             near(off_shape, bf16),

time: 62.3 us -> 61.6 us (0.989)
  Pallas kernels: 6.25 us -> 5.57 us
where the time goes in v3:
time: 61.6 us; the launch traced here: 61.4 us
  blocking collectives  55.8 us (91%)
  Pallas kernels  5.57 us (9%)
    all_to_all x4, blocking collectives, exchange(): return lax.all_to_all(parts, AXES, split_axis=0, concat_axis=0, tiled=True)  55.8 us
    pallas_call x4, Pallas kernels, shards(): pl.pallas_call(functools.partial(later_kernel, level, levels, owners, nam...  3.27 us
    pallas_call x1, Pallas kernels, shards(): pl.pallas_call(functools.partial(first_kernel, owners), out_shape=[near((...  2.3 us

profile of v3, /device:TPU:1, one launch (start us, length us, event | category | flops | bytes accessed | tf_op | source)
XLA Modules:
  0.0 61.4 jit_solution(10466039402396497332)
XLA Ops:
  0.0 0.0 copy-start.1
  0.0 0.0 copy-start.2
  0.0 0.0 copy-start
  0.0 2.3 %level_0.1 = (f32[544,1,128]{2,1,0:T(1,128)S(1)}, f32[16,8,128]{2,1,0:T(8,128)S(1)}, s32[5]{0:T(128)S(4)}, s32[4,32]{1,0:T(4,128)S(4)}, s32[4,32]{1,0:T(4,128)S(4)}) custom-call(s32[5]{0:T(128)} %bitcast.17, s32[4,32]{1,0:T(4,128)} %refs_1_.5, s32[4,32]{1,0:T(4,128)} %refs_2_.5, s32[4,32]{1,0:T(4,128)} %refs_3_.1, f32[5,16,8,128]{3,2,1,0:T(8,128)} %refs_1_.9, ...), custom_call_target="tpu_custom_call" | custom-call | tf_op jit(solution)/shard_map/level_0/pallas_call | solution.py:208
  2.3 17.7 %all_to_all.20 = f32[32,17,1,128]{3,2,1,0:T(1,128)S(1)} all-to-all(f32[32,17,1,128]{3,2,1,0:T(1,128)S(1)} %bitcast.13), channel_id=1, replica_groups=mesh['gx'=4,'gy'=4,'gz'=2] {'gx','gy','gz'}, dimensions={0} | all-to-all | bytes 557056 | tf_op jit(solution)/shard_map/all_to_all | solution.py:206
  20.0 0.0 copy-done.1
  20.0 0.0 copy-done.2
  20.0 0.0 copy-done
  20.0 0.9 %level_1.1 = (f32[5,16,8,128]{3,2,1,0:T(8,128)}, s32[8,32]{1,0:T(8,128)S(4)}, f32[16,8,128]{2,1,0:T(8,128)S(1)}, f32[64,8,128]{2,1,0:T(8,128)S(1)}, f32[48,8,128]{2,1,0:T(8,128)S(1)}) custom-call(s32[5]{0:T(128)S(4)} %get-tuple-element.23.refs_0_, f32[5,16,8,128]{3,2,1,0:T(8,128)S(1)} %copy-done.2, bf16[5,16,128,128]{3,2,1,0:T(8,128)(2,1)S(1)} %copy-done.1, ...), custom_call_target="tpu_custom_call" | custom-call | tf_op jit(solution)/shard_map/level_1/pallas_call | solution.py:257
  20.9 12.7 %all_to_all.21 = f32[32,16,128]{2,1,0:T(8,128)S(1)} all-to-all(f32[32,16,128]{2,1,0:T(8,128)S(1)} %bitcast.16), channel_id=1, replica_groups=mesh['gx'=4,'gy'=4,'gz'=2] {'gx','gy','gz'}, dimensions={0} | all-to-all | bytes 524288 | tf_op jit(solution)/shard_map/all_to_all | solution.py:206
  33.6 0.7 %level_2.1 = (f32[5,16,8,128]{3,2,1,0:T(8,128)}, f32[16,8,128]{2,1,0:T(8,128)S(1)}, f32[64,8,128]{2,1,0:T(8,128)S(1)}, f32[32,8,128]{2,1,0:T(8,128)S(1)}) custom-call(s32[5]{0:T(128)S(4)} %get-tuple-element.23.refs_0_, f32[5,16,8,128]{3,2,1,0:T(8,128)S(1)} %copy-done.2, bf16[5,16,128,128]{3,2,1,0:T(8,128)(2,1)S(1)} %copy-done.1, ...), custom_call_target="tpu_custom_call", output_to_operand_aliasing={{0}: (10, {})} | custom-call | tf_op jit(solution)/shard_map/level_2/pallas_call | solution.py:257
  34.3 12.7 %all_to_all.22 = f32[32,16,128]{2,1,0:T(8,128)S(1)} all-to-all(f32[32,16,128]{2,1,0:T(8,128)S(1)} %bitcast.15), channel_id=1, replica_groups=mesh['gx'=4,'gy'=4,'gz'=2] {'gx','gy','gz'}, dimensions={0} | all-to-all | bytes 524288 | tf_op jit(solution)/shard_map/all_to_all | solution.py:206
  47.0 0.7 %level_3.1 = (f32[5,16,8,128]{3,2,1,0:T(8,128)}, f32[16,8,128]{2,1,0:T(8,128)S(1)}, f32[64,8,128]{2,1,0:T(8,128)S(1)}, f32[16,8,128]{2,1,0:T(8,128)S(1)}) custom-call(s32[5]{0:T(128)S(4)} %get-tuple-element.23.refs_0_, f32[5,16,8,128]{3,2,1,0:T(8,128)S(1)} %copy-done.2, bf16[5,16,128,128]{3,2,1,0:T(8,128)(2,1)S(1)} %copy-done.1, ...), custom_call_target="tpu_custom_call", output_to_operand_aliasing={{0}: (10, {})} | custom-call | tf_op jit(solution)/shard_map/level_3/pallas_call | solution.py:257
  47.7 12.7 %all_to_all.23 = f32[32,16,128]{2,1,0:T(8,128)S(1)} all-to-all(f32[32,16,128]{2,1,0:T(8,128)S(1)} %bitcast.14), channel_id=1, replica_groups=mesh['gx'=4,'gy'=4,'gz'=2] {'gx','gy','gz'}, dimensions={0} | all-to-all | bytes 524288 | tf_op jit(solution)/shard_map/all_to_all | solution.py:206
  60.3 1.1 %level_4.1 = f32[5,16,8,128]{3,2,1,0:T(8,128)} custom-call(s32[5]{0:T(128)S(4)} %get-tuple-element.23.refs_0_, f32[5,16,8,128]{3,2,1,0:T(8,128)S(1)} %copy-done.2, bf16[5,16,128,128]{3,2,1,0:T(8,128)(2,1)S(1)} %copy-done.1, f32[64,8,128]{2,1,0:T(8,128)S(1)} %bitcast.12, f32[16,8,128]{2,1,0:T(8,128)S(1)} %get-tuple-element.38.refs_4_, ...), custom_call_target="tpu_custom_call", output_to_operand_aliasing={{}: (7, {})} | custom-call | tf_op jit(solution)/shard_map/level_4/pallas_call | solution.py:257
Async XLA Ops:
  0.0 20.0 %copy-start.1 = (bf16[5,16,128,128]{3,2,1,0:T(8,128)(2,1)S(1)}, bf16[5,16,128,128]{3,2,1,0:T(8,128)(2,1)}, u32[]{:S(2)}) copy-start(bf16[5,16,128,128]{3,2,1,0:T(8,128)(2,1)} %refs_2_.9) | copy-start | bytes 7864324
  0.0 20.0 %copy-start.2 = (f32[5,16,8,128]{3,2,1,0:T(8,128)S(1)}, f32[5,16,8,128]{3,2,1,0:T(8,128)}, u32[]{:S(2)}) copy-start(f32[5,16,8,128]{3,2,1,0:T(8,128)} %refs_1_.9) | copy-start | bytes 983044
  0.0 20.0 %copy-start = (bf16[4,32,128,128]{3,2,1,0:T(8,128)(2,1)S(1)}, bf16[4,32,128,128]{3,2,1,0:T(8,128)(2,1)}, u32[]{:S(2)}) copy-start(bf16[4,32,128,128]{3,2,1,0:T(8,128)(2,1)} %refs_9_.3) | copy-start | bytes 12582916

commit v4 on v3

--- a/solution.py
+++ b/solution.py
@@ -13,7 +13,6 @@
 SMEM = pl.BlockSpec(memory_space=pltpu.SMEM)
 HBM = pl.BlockSpec(memory_space=pltpu.HBM)
 PARAMS = pltpu.CompilerParams(vmem_limit_bytes=16 * 1024 * 1024)
-PIECES = 4
 
 
 class Copies:
@@ -33,11 +32,6 @@
 def wait(*copies):
     for copy in copies:
         copy.wait()
-
-
-def pieces(count):
-    size = -(-count // (2 * PIECES)) * 2
-    return [(at, min(size, count - at)) for at in range(0, count, size)]
 
 
 def products(left, blocks, start, count):
@@ -67,15 +61,14 @@
     owner_rows, block_rows, place_rows, rhs_now, diag_now, off_now, sems = refs[12:]
     copies = Copies(sems)
     tables = [copies.start(target, owner_rows), copies.start(block, block_rows)]
-    scalars = [copies.start(source, source_now), copies.start(live, live_now)]
+    load_diag = copies.start(diag.at[0], diag_now)
     load_rhs = copies.start(rhs.at[0], rhs_now)
-    load_diag = copies.start(diag.at[0], diag_now)
+    scalars = [copies.start(live, live_now), copies.start(source, source_now)]
     steps, records = owner_rows.shape
     slots, rows, width = solved.shape
     chunk = CAP * rows + 1
     out = outgoing.reshape(owners * chunk, width)
-    parts = pieces(records)
-    load_off = [copies.start(off.at[0, pl.ds(at, size)], off_now.at[pl.ds(at, size)]) for at, size in parts]
+    load_off = copies.start(off.at[0], off_now)
     wait(*tables)
 
     blocks = (steps + 1) * slots
@@ -104,12 +97,14 @@
 
     wait(load_rhs, load_diag, *scalars)
     solve(live_now[0], lambda slot: rhs_now[slot], diag_now, solved)
-    keep_place.wait()
-    for (at, size), copy in zip(parts, load_off):
-        copy.wait()
-        values = products(lambda i: solved[source_now[0, at + i]], off_now, at, size)
-        for record, value in enumerate(values, at):
-            out[pl.ds(place[0, record], rows), :] = value
+    wait(keep_place, load_off)
+    values = products(lambda i: solved[source_now[0, i]], off_now, 0, records)
+    for record, value in enumerate(values):
+        out[pl.ds(place[0, record], rows), :] = value
+
+
+def chains(level):
+    return [f"total_{at}" for at in range(2 if level == 1 else 4)]
 
 
 def add_arrived(level, levels, owners, at, keep_labels):
@@ -117,19 +112,19 @@
     slots, rows, width = at["solved"].shape
     left = levels - level
     chunk = CAP * rows
-    totals = at["even"], at["odd"]
+    totals = [at[name] for name in chains(level)]
+    for total in totals:
+        total[...] = jnp.zeros_like(total)
     if level == 1:
         flat = at["arrived"].reshape(owners * (chunk + 1), width)
-        totals[0][...] = jnp.zeros_like(totals[0])
-        totals[1][...] = jnp.zeros_like(totals[1])
     else:
         totals[0][0 : left * slots] = at["before"][...]
-        totals[1][...] = jnp.zeros_like(totals[1])
     for owner in range(owners):
         if level == 1:
             row = owner * (chunk + 1) + chunk
             sent = flat[row : row + 1, :].astype(jnp.int32) - level * slots
-        for which, total in enumerate(totals):
+        for which in range(CAP):
+            total = totals[(owner * CAP + which) % len(totals)]
             if level == 1:
                 label = sent[0, which]
             else:
@@ -150,12 +145,17 @@
 
 
 def solve_and_pack(level, levels, at, copies):
-    solved, live, totals = at["solved"], at["live"], (at["even"], at["odd"])
+    solved, live = at["solved"], at["live"]
     slots = solved.shape[0]
     last = level == levels - 1
     left = levels - level
     rhs = at["rhs"].at[level]
-    solve(live[level], lambda slot: rhs[slot] - (totals[0][slot] + totals[1][slot]), at["diag"].at[level], solved)
+    totals = [at[name] for name in chains(level)]
+
+    def total_of(part):
+        return sum((total[part] for total in totals[1:]), totals[0][part])
+
+    solve(live[level], lambda slot: rhs[slot] - total_of(slot), at["diag"].at[level], solved)
     if last:
         wait(copies.start(solved, at["answer"].at[level]))
     else:
@@ -163,14 +163,16 @@
         values = products(lambda i: solved[at["source"][level, i]], off, 0, off.shape[0])
         for record, value in enumerate(values):
             at["outgoing"][at["place"][level, record]] = value
-        at["after"][...] = totals[0][slots : left * slots] + totals[1][slots : left * slots]
+        at["after"][...] = total_of(slice(slots, left * slots))
 
 
 def later_kernel(level, levels, owners, names, *refs):
     at = dict(zip(names, refs))
     copies = Copies(at["sems"])
     live = at["live"]
-    ahead = [copies.start(at["solved_before"], at["answer"].at[level - 1])]
+    ahead = []
+    if level == levels - 1:
+        ahead = [copies.start(at[f"solved_{before}"], at["answer"].at[before]) for before in range(level)]
 
     keep_labels = copies.make(at["turned"], at["labels"]) if level == 1 else None
 
@@ -223,52 +225,51 @@
             near(rows_shape, f32),
             near(diag_shape, bf16),
             near(off_shape, bf16),
-            semaphores((11 + PIECES,)),
+            semaphores((8,)),
         ],
         name="level_0",
         compiler_params=PARAMS,
     )(*arguments)
     arrived = exchange(outgoing.reshape(owners, chunk + 1, 1, width)).reshape(owners * (chunk + 1), 1, width)
 
-    answer = labels = before = None
+    solved = [solved]
+    labels = before = None
     for level in range(1, levels):
         last = level == levels - 1
         left = levels - level
         ins = [("live", live, SMEM), ("rhs", rhs, VMEM), ("diag", diag, VMEM), ("arrived", arrived, VMEM)]
-        ins.append(("solved_before", solved, VMEM))
-        outs = [("answer", pltpu.HBM((levels, *rows_shape), f32), HBM)]
-        scratch = [("even", near((left * slots + 1, rows, width), f32)), ("odd", near((left * slots + 1, rows, width), f32))]
-        scratch.append(("sems", semaphores((6,))))
+        outs = []
+        scratch = [(name, near((left * slots + 1, rows, width), f32)) for name in chains(level)]
+        scratch.append(("sems", semaphores((levels + 1,))))
         if level == 1:
             outs.append(("labels", table((steps * CAP, owners), i32), SMEM))
             scratch += [("gathered", near((owners, width), f32)), ("turned", near((steps * CAP, owners), i32))]
         else:
             ins += [("labels", labels, SMEM), ("before", before, VMEM)]
         if last:
+            ins += [(f"solved_{before}", value, VMEM) for before, value in enumerate(solved)]
+            outs.append(("answer", pltpu.HBM((levels, *rows_shape), f32), HBM))
             scratch.append(("solved", near(rows_shape, f32)))
         else:
             ins += [("source", source, SMEM), ("place", place, SMEM), ("off", off, VMEM)]
             outs.append(("solved", near(rows_shape, f32), VMEM))
             outs.append(("outgoing", near((owners * CAP, rows, width), f32), VMEM))
             outs.append(("after", near(((left - 1) * slots, rows, width), f32), VMEM))
-        if level > 1:
-            ins.append(("answer_before", pltpu.with_memory_space_constraint(answer, pltpu.HBM), HBM))
         names = [name for name, *_ in ins + outs + scratch]
         made = pl.pallas_call(
             functools.partial(later_kernel, level, levels, owners, names),
             out_shape=[shape for _, shape, _ in outs],
             in_specs=[spec for *_, spec in ins],
             out_specs=[spec for *_, spec in outs],
-            input_output_aliases={len(ins) - 1: 0} if level > 1 else {},
             scratch_shapes=[shape for _, shape in scratch],
             name=f"level_{level}",
             compiler_params=PARAMS,
         )(*[value for _, value, _ in ins])
         made = dict(zip([name for name, *_ in outs], made))
-        answer = made["answer"]
         if last:
-            return answer
-        solved, before = made["solved"], made["after"]
+            return made["answer"]
+        solved.append(made["solved"])
+        before = made["after"]
         labels = made.get("labels", labels)
         arrived = exchange(made["outgoing"].reshape(owners, chunk, width)).reshape(owners * CAP, rows, width)
 

time: 61.6 us -> 61 us (level)
  no operation moved by 1% of the time
where the time goes in v4:
time: 61 us; the launch traced here: 60.8 us
  blocking collectives  55.8 us (91%)
  Pallas kernels  5 us (8%)
    all_to_all x4, blocking collectives, exchange(): return lax.all_to_all(parts, AXES, split_axis=0, concat_axis=0, tiled=True)  55.8 us
    pallas_call x4, Pallas kernels, shards(): pl.pallas_call(functools.partial(later_kernel, level, levels, owners, nam...  3.08 us
    pallas_call x1, Pallas kernels, shards(): pl.pallas_call(functools.partial(first_kernel, owners), out_shape=[near((...  1.91 us

profile of v4, /device:TPU:1, one launch (start us, length us, event | category | flops | bytes accessed | tf_op | source)
XLA Modules:
  0.0 60.8 jit_solution(18051728257866628017)
XLA Ops:
  0.0 0.0 copy-start.1
  0.0 0.0 copy-start.2
  0.0 0.0 copy-start
  0.0 1.9 %level_0.1 = (f32[544,1,128]{2,1,0:T(1,128)S(1)}, f32[16,8,128]{2,1,0:T(8,128)S(1)}, s32[5]{0:T(128)S(4)}, s32[4,32]{1,0:T(4,128)S(4)}, s32[4,32]{1,0:T(4,128)S(4)}) custom-call(s32[5]{0:T(128)} %bitcast.17, s32[4,32]{1,0:T(4,128)} %refs_1_.5, s32[4,32]{1,0:T(4,128)} %refs_2_.5, s32[4,32]{1,0:T(4,128)} %refs_3_.1, f32[5,16,8,128]{3,2,1,0:T(8,128)} %refs_1_.9, ...), custom_call_target="tpu_custom_call" | custom-call | tf_op jit(solution)/shard_map/level_0/pallas_call | solution.py:210
  1.9 17.7 %all_to_all.20 = f32[32,17,1,128]{3,2,1,0:T(1,128)S(1)} all-to-all(f32[32,17,1,128]{3,2,1,0:T(1,128)S(1)} %bitcast.13), channel_id=1, replica_groups=mesh['gx'=4,'gy'=4,'gz'=2] {'gx','gy','gz'}, dimensions={0} | all-to-all | bytes 557056 | tf_op jit(solution)/shard_map/all_to_all | solution.py:208
  19.6 0.0 copy-done.1
  19.7 0.0 copy-done.2
  19.7 0.0 copy-done
  19.7 0.9 %level_1.1 = (s32[8,32]{1,0:T(8,128)S(4)}, f32[16,8,128]{2,1,0:T(8,128)S(1)}, f32[64,8,128]{2,1,0:T(8,128)S(1)}, f32[48,8,128]{2,1,0:T(8,128)S(1)}) custom-call(s32[5]{0:T(128)S(4)} %get-tuple-element.20.refs_0_, f32[5,16,8,128]{3,2,1,0:T(8,128)S(1)} %copy-done.2, bf16[5,16,128,128]{3,2,1,0:T(8,128)(2,1)S(1)} %copy-done.1, f32[544,1,128]{2,1,0:T(1,128)S(1)} %bitcast.9, ...), custom_call_target="tpu_custom_call" | custom-call | tf_op jit(solution)/shard_map/level_1/pallas_call | solution.py:259
  20.5 12.7 %all_to_all.21 = f32[32,16,128]{2,1,0:T(8,128)S(1)} all-to-all(f32[32,16,128]{2,1,0:T(8,128)S(1)} %bitcast.15), channel_id=1, replica_groups=mesh['gx'=4,'gy'=4,'gz'=2] {'gx','gy','gz'}, dimensions={0} | all-to-all | bytes 524288 | tf_op jit(solution)/shard_map/all_to_all | solution.py:208
  33.2 0.6 %level_2.1 = (f32[16,8,128]{2,1,0:T(8,128)S(1)}, f32[64,8,128]{2,1,0:T(8,128)S(1)}, f32[32,8,128]{2,1,0:T(8,128)S(1)}) custom-call(s32[5]{0:T(128)S(4)} %get-tuple-element.20.refs_0_, f32[5,16,8,128]{3,2,1,0:T(8,128)S(1)} %copy-done.2, bf16[5,16,128,128]{3,2,1,0:T(8,128)(2,1)S(1)} %copy-done.1, f32[64,8,128]{2,1,0:T(8,128)S(1)} %bitcast.12, ...), custom_call_target="tpu_custom_call" | custom-call | tf_op jit(solution)/shard_map/level_2/pallas_call | solution.py:259
  33.9 12.7 %all_to_all.22 = f32[32,16,128]{2,1,0:T(8,128)S(1)} all-to-all(f32[32,16,128]{2,1,0:T(8,128)S(1)} %bitcast.16), channel_id=1, replica_groups=mesh['gx'=4,'gy'=4,'gz'=2] {'gx','gy','gz'}, dimensions={0} | all-to-all | bytes 524288 | tf_op jit(solution)/shard_map/all_to_all | solution.py:208
  46.5 0.6 level_3.1
  47.2 12.7 %all_to_all.23 = f32[32,16,128]{2,1,0:T(8,128)S(1)} all-to-all(f32[32,16,128]{2,1,0:T(8,128)S(1)} %bitcast.14), channel_id=1, replica_groups=mesh['gx'=4,'gy'=4,'gz'=2] {'gx','gy','gz'}, dimensions={0} | all-to-all | bytes 524288 | tf_op jit(solution)/shard_map/all_to_all | solution.py:208
  59.8 1.0 %level_4.1 = f32[5,16,8,128]{3,2,1,0:T(8,128)} custom-call(s32[5]{0:T(128)S(4)} %get-tuple-element.20.refs_0_, f32[5,16,8,128]{3,2,1,0:T(8,128)S(1)} %copy-done.2, bf16[5,16,128,128]{3,2,1,0:T(8,128)(2,1)S(1)} %copy-done.1, f32[64,8,128]{2,1,0:T(8,128)S(1)} %bitcast.10, s32[8,32]{1,0:T(8,128)S(4)} %get-tuple-element.25.refs_4_, ...), custom_call_target="tpu_custom_call" | custom-call | tf_op jit(solution)/shard_map/level_4/pallas_call | solution.py:259
Async XLA Ops:
  0.0 19.7 %copy-start.1 = (bf16[5,16,128,128]{3,2,1,0:T(8,128)(2,1)S(1)}, bf16[5,16,128,128]{3,2,1,0:T(8,128)(2,1)}, u32[]{:S(2)}) copy-start(bf16[5,16,128,128]{3,2,1,0:T(8,128)(2,1)} %refs_2_.9) | copy-start | bytes 7864324
  0.0 19.7 %copy-start.2 = (f32[5,16,8,128]{3,2,1,0:T(8,128)S(1)}, f32[5,16,8,128]{3,2,1,0:T(8,128)}, u32[]{:S(2)}) copy-start(f32[5,16,8,128]{3,2,1,0:T(8,128)} %refs_1_.9) | copy-start | bytes 983044
  0.0 19.7 %copy-start = (bf16[4,32,128,128]{3,2,1,0:T(8,128)(2,1)S(1)}, bf16[4,32,128,128]{3,2,1,0:T(8,128)(2,1)}, u32[]{:S(2)}) copy-start(bf16[4,32,128,128]{3,2,1,0:T(8,128)(2,1)} %refs_8_.3) | copy-start | bytes 12582916

commit v5 on v4

--- a/solution.py
+++ b/solution.py
@@ -91,7 +91,8 @@
             label = (value.astype(jnp.int32) & (base - 1)).astype(jnp.float32)
             label = jnp.where(low < none, label, jnp.float32(blocks))
             labels = jnp.where(lane == level * CAP + at, label, labels)
-    keep_place = copies.start(place_rows, place)
+    keep_place = pltpu.make_async_copy(place_rows, place, sems.at[0])
+    keep_place.start()
     for owner in range(owners):
         out[owner * chunk + CAP * rows : (owner + 1) * chunk, :] = labels[owner : owner + 1, :]
 
@@ -168,7 +169,7 @@
 
 def later_kernel(level, levels, owners, names, *refs):
     at = dict(zip(names, refs))
-    copies = Copies(at["sems"])
+    copies = Copies(at.get("sems"))
     live = at["live"]
     ahead = []
     if level == levels - 1:
@@ -225,7 +226,7 @@
             near(rows_shape, f32),
             near(diag_shape, bf16),
             near(off_shape, bf16),
-            semaphores((8,)),
+            semaphores((7,)),
         ],
         name="level_0",
         compiler_params=PARAMS,
@@ -240,7 +241,8 @@
         ins = [("live", live, SMEM), ("rhs", rhs, VMEM), ("diag", diag, VMEM), ("arrived", arrived, VMEM)]
         outs = []
         scratch = [(name, near((left * slots + 1, rows, width), f32)) for name in chains(level)]
-        scratch.append(("sems", semaphores((levels + 1,))))
+        if level == 1 or last:
+            scratch.append(("sems", semaphores((levels if last else 1,))))
         if level == 1:
             outs.append(("labels", table((steps * CAP, owners), i32), SMEM))
             scratch += [("gathered", near((owners, width), f32)), ("turned", near((steps * CAP, owners), i32))]

time: 61 us -> 60.8 us (level)
  no operation moved by 1% of the time
where the time goes in v5:
time: 60.8 us; the launch traced here: 60.6 us
  blocking collectives  55.8 us (92%)
  Pallas kernels  4.8 us (8%)
    all_to_all x4, blocking collectives, exchange(): return lax.all_to_all(parts, AXES, split_axis=0, concat_axis=0, tiled=True)  55.8 us
    pallas_call x4, Pallas kernels, shards(): pl.pallas_call(functools.partial(later_kernel, level, levels, owners, nam...  2.89 us
    pallas_call x1, Pallas kernels, shards(): pl.pallas_call(functools.partial(first_kernel, owners), out_shape=[near((...  1.9 us

profile of v5, /device:TPU:1, one launch (start us, length us, event | category | flops | bytes accessed | tf_op | source)
XLA Modules:
  0.0 60.6 jit_solution(15699348105556103744)
XLA Ops:
  0.0 0.0 copy-start.1
  0.0 0.0 copy-start.2
  0.0 0.0 copy-start
  0.0 1.9 %level_0.1 = (f32[544,1,128]{2,1,0:T(1,128)S(1)}, f32[16,8,128]{2,1,0:T(8,128)S(1)}, s32[5]{0:T(128)S(4)}, s32[4,32]{1,0:T(4,128)S(4)}, s32[4,32]{1,0:T(4,128)S(4)}) custom-call(s32[5]{0:T(128)} %bitcast.17, s32[4,32]{1,0:T(4,128)} %refs_1_.5, s32[4,32]{1,0:T(4,128)} %refs_2_.5, s32[4,32]{1,0:T(4,128)} %refs_3_.1, f32[5,16,8,128]{3,2,1,0:T(8,128)} %refs_1_.9, ...), custom_call_target="tpu_custom_call" | custom-call | tf_op jit(solution)/shard_map/level_0/pallas_call | solution.py:211
  1.9 17.7 %all_to_all.20 = f32[32,17,1,128]{3,2,1,0:T(1,128)S(1)} all-to-all(f32[32,17,1,128]{3,2,1,0:T(1,128)S(1)} %bitcast.13), channel_id=1, replica_groups=mesh['gx'=4,'gy'=4,'gz'=2] {'gx','gy','gz'}, dimensions={0} | all-to-all | bytes 557056 | tf_op jit(solution)/shard_map/all_to_all | solution.py:209
  19.6 0.0 copy-done.1
  19.6 0.0 copy-done.2
  19.6 0.0 copy-done
  19.6 0.8 %level_1.1 = (s32[8,32]{1,0:T(8,128)S(4)}, f32[16,8,128]{2,1,0:T(8,128)S(1)}, f32[64,8,128]{2,1,0:T(8,128)S(1)}, f32[48,8,128]{2,1,0:T(8,128)S(1)}) custom-call(s32[5]{0:T(128)S(4)} %get-tuple-element.20.refs_0_, f32[5,16,8,128]{3,2,1,0:T(8,128)S(1)} %copy-done.2, bf16[5,16,128,128]{3,2,1,0:T(8,128)(2,1)S(1)} %copy-done.1, f32[544,1,128]{2,1,0:T(1,128)S(1)} %bitcast.9, ...), custom_call_target="tpu_custom_call" | custom-call | tf_op jit(solution)/shard_map/level_1/pallas_call | solution.py:261
  20.5 12.7 %all_to_all.21 = f32[32,16,128]{2,1,0:T(8,128)S(1)} all-to-all(f32[32,16,128]{2,1,0:T(8,128)S(1)} %bitcast.15), channel_id=1, replica_groups=mesh['gx'=4,'gy'=4,'gz'=2] {'gx','gy','gz'}, dimensions={0} | all-to-all | bytes 524288 | tf_op jit(solution)/shard_map/all_to_all | solution.py:209
  33.2 0.6 level_2.1
  33.7 12.7 %all_to_all.22 = f32[32,16,128]{2,1,0:T(8,128)S(1)} all-to-all(f32[32,16,128]{2,1,0:T(8,128)S(1)} %bitcast.16), channel_id=1, replica_groups=mesh['gx'=4,'gy'=4,'gz'=2] {'gx','gy','gz'}, dimensions={0} | all-to-all | bytes 524288 | tf_op jit(solution)/shard_map/all_to_all | solution.py:209
  46.4 0.5 level_3.1
  47.0 12.7 %all_to_all.23 = f32[32,16,128]{2,1,0:T(8,128)S(1)} all-to-all(f32[32,16,128]{2,1,0:T(8,128)S(1)} %bitcast.14), channel_id=1, replica_groups=mesh['gx'=4,'gy'=4,'gz'=2] {'gx','gy','gz'}, dimensions={0} | all-to-all | bytes 524288 | tf_op jit(solution)/shard_map/all_to_all | solution.py:209
  59.6 1.0 %level_4.1 = f32[5,16,8,128]{3,2,1,0:T(8,128)} custom-call(s32[5]{0:T(128)S(4)} %get-tuple-element.20.refs_0_, f32[5,16,8,128]{3,2,1,0:T(8,128)S(1)} %copy-done.2, bf16[5,16,128,128]{3,2,1,0:T(8,128)(2,1)S(1)} %copy-done.1, f32[64,8,128]{2,1,0:T(8,128)S(1)} %bitcast.10, s32[8,32]{1,0:T(8,128)S(4)} %get-tuple-element.25.refs_4_, ...), custom_call_target="tpu_custom_call" | custom-call | tf_op jit(solution)/shard_map/level_4/pallas_call | solution.py:261
Async XLA Ops:
  0.0 19.6 %copy-start.1 = (bf16[5,16,128,128]{3,2,1,0:T(8,128)(2,1)S(1)}, bf16[5,16,128,128]{3,2,1,0:T(8,128)(2,1)}, u32[]{:S(2)}) copy-start(bf16[5,16,128,128]{3,2,1,0:T(8,128)(2,1)} %refs_2_.9) | copy-start | bytes 7864324
  0.0 19.6 %copy-start.2 = (f32[5,16,8,128]{3,2,1,0:T(8,128)S(1)}, f32[5,16,8,128]{3,2,1,0:T(8,128)}, u32[]{:S(2)}) copy-start(f32[5,16,8,128]{3,2,1,0:T(8,128)} %refs_1_.9) | copy-start | bytes 983044
  0.0 19.6 %copy-start = (bf16[4,32,128,128]{3,2,1,0:T(8,128)(2,1)S(1)}, bf16[4,32,128,128]{3,2,1,0:T(8,128)(2,1)}, u32[]{:S(2)}) copy-start(bf16[4,32,128,128]{3,2,1,0:T(8,128)(2,1)} %refs_8_.3) | copy-start | bytes 12582916

commit v6 on v5

--- a/solution.py
+++ b/solution.py
@@ -177,13 +177,20 @@
 
     keep_labels = copies.make(at["turned"], at["labels"]) if level == 1 else None
 
-    @pl.when(live[level] >= 0)
-    def _():
+    def region(work):
+        if level == 1 or level == levels - 1:
+            pl.when(live[level] >= 0)(work)
+        else:
+            work()
+
+    def add():
         add_arrived(level, levels, owners, at, keep_labels)
-
-    @pl.when(live[level] >= 0)
-    def _():
-        solve_and_pack(level, levels, at, copies)
+        if level > 1:
+            solve_and_pack(level, levels, at, copies)
+
+    region(add)
+    if level == 1:
+        region(lambda: solve_and_pack(level, levels, at, copies))
 
     wait(*ahead, *([keep_labels] if level == 1 else []))
 

time: 60.8 us -> 60.8 us (level)
  no operation moved by 1% of the time
where the time goes in v6:
time: 60.8 us; the launch traced here: 60.6 us
  blocking collectives  55.8 us (92%)
  Pallas kernels  4.82 us (8%)
    all_to_all x4, blocking collectives, exchange(): return lax.all_to_all(parts, AXES, split_axis=0, concat_axis=0, tiled=True)  55.8 us
    pallas_call x4, Pallas kernels, shards(): pl.pallas_call(functools.partial(later_kernel, level, levels, owners, nam...  2.92 us
    pallas_call x1, Pallas kernels, shards(): pl.pallas_call(functools.partial(first_kernel, owners), out_shape=[near((...  1.9 us

profile of v6, /device:TPU:1, one launch (start us, length us, event | category | flops | bytes accessed | tf_op | source)
XLA Modules:
  0.0 60.6 jit_solution(13862842646371280815)
XLA Ops:
  0.0 0.0 copy-start.1
  0.0 0.0 copy-start.2
  0.0 0.0 copy-start
  0.0 1.9 %level_0.1 = (f32[544,1,128]{2,1,0:T(1,128)S(1)}, f32[16,8,128]{2,1,0:T(8,128)S(1)}, s32[5]{0:T(128)S(4)}, s32[4,32]{1,0:T(4,128)S(4)}, s32[4,32]{1,0:T(4,128)S(4)}) custom-call(s32[5]{0:T(128)} %bitcast.17, s32[4,32]{1,0:T(4,128)} %refs_1_.5, s32[4,32]{1,0:T(4,128)} %refs_2_.5, s32[4,32]{1,0:T(4,128)} %refs_3_.1, f32[5,16,8,128]{3,2,1,0:T(8,128)} %refs_1_.9, ...), custom_call_target="tpu_custom_call" | custom-call | tf_op jit(solution)/shard_map/level_0/pallas_call | solution.py:218
  1.9 17.7 %all_to_all.20 = f32[32,17,1,128]{3,2,1,0:T(1,128)S(1)} all-to-all(f32[32,17,1,128]{3,2,1,0:T(1,128)S(1)} %bitcast.13), channel_id=1, replica_groups=mesh['gx'=4,'gy'=4,'gz'=2] {'gx','gy','gz'}, dimensions={0} | all-to-all | bytes 557056 | tf_op jit(solution)/shard_map/all_to_all | solution.py:216
  19.6 0.0 copy-done.1
  19.6 0.0 copy-done.2
  19.6 0.0 copy-done
  19.7 0.8 %level_1.1 = (s32[8,32]{1,0:T(8,128)S(4)}, f32[16,8,128]{2,1,0:T(8,128)S(1)}, f32[64,8,128]{2,1,0:T(8,128)S(1)}, f32[48,8,128]{2,1,0:T(8,128)S(1)}) custom-call(s32[5]{0:T(128)S(4)} %get-tuple-element.20.refs_0_, f32[5,16,8,128]{3,2,1,0:T(8,128)S(1)} %copy-done.2, bf16[5,16,128,128]{3,2,1,0:T(8,128)(2,1)S(1)} %copy-done.1, f32[544,1,128]{2,1,0:T(1,128)S(1)} %bitcast.9, ...), custom_call_target="tpu_custom_call" | custom-call | tf_op jit(solution)/shard_map/level_1/pallas_call | solution.py:268
  20.5 12.7 %all_to_all.21 = f32[32,16,128]{2,1,0:T(8,128)S(1)} all-to-all(f32[32,16,128]{2,1,0:T(8,128)S(1)} %bitcast.15), channel_id=1, replica_groups=mesh['gx'=4,'gy'=4,'gz'=2] {'gx','gy','gz'}, dimensions={0} | all-to-all | bytes 524288 | tf_op jit(solution)/shard_map/all_to_all | solution.py:216
  33.2 0.6 level_2.1
  33.8 12.7 %all_to_all.22 = f32[32,16,128]{2,1,0:T(8,128)S(1)} all-to-all(f32[32,16,128]{2,1,0:T(8,128)S(1)} %bitcast.16), channel_id=1, replica_groups=mesh['gx'=4,'gy'=4,'gz'=2] {'gx','gy','gz'}, dimensions={0} | all-to-all | bytes 524288 | tf_op jit(solution)/shard_map/all_to_all | solution.py:216
  46.4 0.5 level_3.1
  47.0 12.7 %all_to_all.23 = f32[32,16,128]{2,1,0:T(8,128)S(1)} all-to-all(f32[32,16,128]{2,1,0:T(8,128)S(1)} %bitcast.14), channel_id=1, replica_groups=mesh['gx'=4,'gy'=4,'gz'=2] {'gx','gy','gz'}, dimensions={0} | all-to-all | bytes 524288 | tf_op jit(solution)/shard_map/all_to_all | solution.py:216
  59.7 1.0 %level_4.1 = f32[5,16,8,128]{3,2,1,0:T(8,128)} custom-call(s32[5]{0:T(128)S(4)} %get-tuple-element.20.refs_0_, f32[5,16,8,128]{3,2,1,0:T(8,128)S(1)} %copy-done.2, bf16[5,16,128,128]{3,2,1,0:T(8,128)(2,1)S(1)} %copy-done.1, f32[64,8,128]{2,1,0:T(8,128)S(1)} %bitcast.10, s32[8,32]{1,0:T(8,128)S(4)} %get-tuple-element.25.refs_4_, ...), custom_call_target="tpu_custom_call" | custom-call | tf_op jit(solution)/shard_map/level_4/pallas_call | solution.py:268
Async XLA Ops:
  0.0 19.6 %copy-start.1 = (bf16[5,16,128,128]{3,2,1,0:T(8,128)(2,1)S(1)}, bf16[5,16,128,128]{3,2,1,0:T(8,128)(2,1)}, u32[]{:S(2)}) copy-start(bf16[5,16,128,128]{3,2,1,0:T(8,128)(2,1)} %refs_2_.9) | copy-start | bytes 7864324
  0.0 19.6 %copy-start.2 = (f32[5,16,8,128]{3,2,1,0:T(8,128)S(1)}, f32[5,16,8,128]{3,2,1,0:T(8,128)}, u32[]{:S(2)}) copy-start(f32[5,16,8,128]{3,2,1,0:T(8,128)} %refs_1_.9) | copy-start | bytes 983044
  0.0 19.6 %copy-start = (bf16[4,32,128,128]{3,2,1,0:T(8,128)(2,1)S(1)}, bf16[4,32,128,128]{3,2,1,0:T(8,128)(2,1)}, u32[]{:S(2)}) copy-start(bf16[4,32,128,128]{3,2,1,0:T(8,128)(2,1)} %refs_8_.3) | copy-start | bytes 12582916
